TPU v7x, 32 devices: a whole 2x2x4 slice. The times are simulated.
32 devices in a mesh: tilt: 2 (over y), row: 8 (over z, x), col: 2 (over core).
Axes of the slice: x: 2, y: 2, z: 4, core: 2. Of those that a mesh axis runs over, the one named last changes fastest.
Arguments:
- object_field: float32 [2, 2048, 256], P(None, ('tilt', 'row'), 'col'), parts along dimension 1, may hold values from -4.2 to 4.2
- probe: float32 [8, 2, 128, 128], P('tilt'), parts along dimension 0, may hold values from -2.1 to 2.1
- patterns: float32 [16, 2, 2, 128, 128], P(('tilt', 'row'), 'col'), parts along dimension 0, may hold values from 0.1 to 3
- offsets: int32 [16, 2, 2, 2], P(('tilt', 'row'), 'col'), parts along dimension 0, may hold values from 0 to 256
- counts: int32 [16, 2], P(('tilt', 'row'), 'col'), parts along dimension 0, may hold values from 1 to 2, as said below
Outputs:
- object_out: float32 [2, 2048, 256], P(None, ('tilt', 'row'), 'col'), parts along dimension 1
- probe_out: float32 [8, 2, 128, 128], P('tilt'), parts along dimension 0
There are 2 independent parts, one for each index of `tilt`. A program takes and returns all parts, laid end to end along the dimension named above; each array names one. Nothing has to cross between parts.
Inputs may be any that keep to these rules, and one draw needn't show every extreme that they name: Only the first counts[r, c] slots of a tile are live; some tile has all 2 live. `offsets`: A window lies inside its tile's frame of 384 pixels a side.
All inputs are finite; a program needn't handle non-finite values.
Results may differ from a plain program's by a relative error of at most 0.0003.
Values sent between devices are 32-bit elements; how exact they have to be, the bound alone decides.
A program may use at most 64 MiB of HBM per device.

v0:
```python
import functools

import jax
import jax.numpy as jnp
import numpy as np
from jax import lax
from jax.experimental import pallas as pl
from jax.experimental.pallas import tpu as pltpu
from jax.sharding import PartitionSpec as P

MESH = pl.DeviceIdType.MESH
F32 = jnp.float32
BF16 = jnp.bfloat16

object_rate = 1.0
probe_rate = 1.0
epsilon = 1e-06


def split_table(table):
    high = table.astype(jnp.bfloat16)
    low = (table - high.astype(np.float64)).astype(jnp.bfloat16)
    return high, low


def dft_tables(length):
    counter = np.arange(length)
    product = counter[:, None] * counter[None, :] % length
    angle = -2.0 * np.pi / length * product
    c, s = np.cos(angle) / np.sqrt(length), np.sin(angle) / np.sqrt(length)
    right = np.block([[c, s], [-s, c]])
    left = right.T
    return np.stack([*split_table(right), *split_table(left)])


def split(x):
    high = x.astype(BF16)
    return high, (x - high.astype(F32)).astype(BF16)


def each_peer(total, step):
    if total <= 16:
        for hop in range(1, total):
            step(hop)
    else:
        lax.fori_loop(1, total, lambda hop, carry: (step(hop), carry)[1], 0)


def dot(a, b):
    return jnp.dot(a, b, preferred_element_type=F32)


def kernel(
    rows, modes, slots, width, owners,
    off_ref, cnt_ref, obj_ref, probe_ref, pat_ref, tab_ref,
    obj_out, probe_out,
    frame, xh, xl, yh, yl, far, vh, vl, win, gacc,
    gown, gpar, grecv, gedge, term, tpart, acc, pieces, red, red_other,
    h_send, h_recv, g_send, g_recv, e_send, e_recv, t_send, t_recv,
    rs_send, rs_recv, ag_send, ag_recv, o_send, o_recv, news,
):
    me = lax.axis_index("row")
    col = lax.axis_index("col")
    n = width
    tiles = rows * 2
    mate = {"col": 1 - col}
    up = {"row": me - 1}
    down = {"row": me + 1}
    has_up, has_down = me > 0, me < rows - 1
    chunk = 2 * n // owners

    def if_row(row, act):
        pl.when(jnp.logical_and(row >= 0, row < rows))(lambda: act({"row": row}))

    def present(distance):
        return (me >= distance).astype(jnp.int32) + (me + distance < rows).astype(jnp.int32)

    barrier = pltpu.get_barrier_semaphore()

    def greet(to):
        pl.semaphore_signal(barrier, inc=1, device_id=to, device_id_type=MESH)

    if_row(me + 1, greet)
    if_row(me - 1, greet)
    greet(mate)
    pl.semaphore_wait(barrier, 1 + present(1))

    rounds = [2]
    while 2 * rounds[-1] < rows:
        rounds.append(2 * rounds[-1])

    def tell(r):
        def act(to):
            pl.semaphore_signal(news.at[r], inc=1, device_id=to, device_id_type=MESH)

        if_row(me - rounds[r], act)
        if_row(me + rounds[r], act)

    def hear(r):
        pl.semaphore_wait(news.at[r], present(rounds[r]))

    def remote(src, dst, send, recv, to):
        return pltpu.make_async_remote_copy(
            src_ref=src, dst_ref=dst, send_sem=send, recv_sem=recv, device_id=to, device_id_type=MESH
        )

    seen = 2 * col
    mine = 2 - 2 * col
    to_mate = remote(obj_ref, frame.at[1, seen], h_send.at[0], h_recv.at[0], mate)
    to_up = remote(obj_ref, frame.at[2, 1], h_send.at[1], h_recv.at[2], up)
    to_down = remote(obj_ref, frame.at[0, 1], h_send.at[2], h_recv.at[1], down)
    relay_up = remote(frame.at[0, 1], frame.at[0, seen], h_send.at[3], h_recv.at[3], mate)
    relay_down = remote(frame.at[2, 1], frame.at[2, seen], h_send.at[4], h_recv.at[4], mate)
    pl.when(has_up)(to_up.start)
    pl.when(has_down)(to_down.start)
    to_mate.start()

    zero = jnp.zeros((2, n, n), F32)
    frame[1, 1] = obj_ref[...]
    for j in range(3):
        frame[j, seen] = zero

    @pl.when(me == 0)
    def _():
        frame[0, 1] = zero
        frame[0, mine] = zero

    @pl.when(me == rows - 1)
    def _():
        frame[2, 1] = zero
        frame[2, mine] = zero

    power = jnp.zeros((n, n), F32)
    for k in range(modes):
        power = power + (probe_ref[k, 0] * probe_ref[k, 0] + probe_ref[k, 1] * probe_ref[k, 1])
    weight = jnp.max(power) + epsilon

    @pl.when(has_up)
    def _():
        to_down.wait_recv()
        relay_up.start()

    @pl.when(has_down)
    def _():
        to_up.wait_recv()
        relay_down.start()

    to_mate.wait_recv()
    pl.when(has_up)(relay_up.wait_recv)
    pl.when(has_down)(relay_down.wait_recv)

    tell(0)

    r_hi, r_lo, l_hi, l_lo = (tab_ref.at[t] for t in range(4))
    row_id = lax.broadcasted_iota(jnp.int32, (n, n), 0)
    lane_id = lax.broadcasted_iota(jnp.int32, (n, n), 1)

    def place(s):
        oy, ox = off_ref[0, 0, s, 0], off_ref[0, 0, s, 1]
        by, bx = oy // n, ox // n
        return by, bx, oy - by * n, ox - bx * n

    for s in range(slots):
        by, bx, sy, sx = place(s)
        by2, bx2 = jnp.minimum(by + 1, 2), jnp.minimum(bx + 1, 2)
        for q in range(2):
            upper = jnp.where(lane_id >= sx, frame[by, bx, q], frame[by, bx2, q])
            lower = jnp.where(lane_id >= sx, frame[by2, bx, q], frame[by2, bx2, q])
            packed = jnp.where(row_id >= sy, upper, lower)
            packed = pltpu.roll(packed, lax.rem(n - sy, n), 0)
            win[s, q] = pltpu.roll(packed, lax.rem(n - sx, n), 1)
        for k in range(modes):
            wr, wi = win[s, 0], win[s, 1]
            pr, pi = probe_ref[k, 0], probe_ref[k, 1]
            for q, part in enumerate((pr * wr - pi * wi, pr * wi + pi * wr)):
                hi, lo = split(part)
                xh[s, k * n : (k + 1) * n, q * n : (q + 1) * n] = hi
                xl[s, k * n : (k + 1) * n, q * n : (q + 1) * n] = lo
        for k in range(modes):
            a_hi, a_lo = xh[s, k * n : (k + 1) * n, :], xl[s, k * n : (k + 1) * n, :]
            y = dot(a_hi, r_hi[...]) + dot(a_lo, r_hi[...]) + dot(a_hi, r_lo[...])
            for q in range(2):
                hi, lo = split(y[:, q * n : (q + 1) * n])
                yh[s, q * n : (q + 1) * n, k * n : (k + 1) * n] = hi
                yl[s, q * n : (q + 1) * n, k * n : (k + 1) * n] = lo
        for p in range(modes // 2):
            cols = slice(2 * p * n, 2 * (p + 1) * n)
            b_hi, b_lo = yh[s, :, cols], yl[s, :, cols]
            far[s, :, cols] = dot(l_hi[...], b_hi) + dot(l_lo[...], b_hi) + dot(l_hi[...], b_lo)
        level = jnp.zeros((n, n), F32)
        for k in range(modes):
            cols = slice(k * n, (k + 1) * n)
            level = level + far[s, :n, cols] * far[s, :n, cols] + far[s, n:, cols] * far[s, n:, cols]
        live = (s < cnt_ref[0, 0]).astype(F32)
        misfit = live * (level - pat_ref[0, 0, s])
        for k in range(modes):
            for q in range(2):
                spot = (s, slice(q * n, (q + 1) * n), slice(k * n, (k + 1) * n))
                hi, lo = split(misfit * far[spot])
                yh[spot] = hi
                yl[spot] = lo

    for r in range(1, len(rounds)):
        hear(r - 1)
        tell(r)

    def to_partner(p):
        return remote(term.at[2 * p + 1 - col], tpart.at[p], t_send.at[p], t_recv.at[p], mate)

    for p in range(modes // 2):
        cols = slice(2 * p * n, 2 * (p + 1) * n)
        for s in range(slots):
            b_hi, b_lo = yh[s, :, cols], yl[s, :, cols]
            v = dot(r_hi[...], b_hi) + dot(r_lo[...], b_hi) + dot(r_hi[...], b_lo)
            for m in range(2):
                for q in range(2):
                    hi, lo = split(v[q * n : (q + 1) * n, m * n : (m + 1) * n])
                    vh[s, m * n : (m + 1) * n, q * n : (q + 1) * n] = hi
                    vl[s, m * n : (m + 1) * n, q * n : (q + 1) * n] = lo
            for m in range(2):
                k = 2 * p + m
                a_hi, a_lo = vh[s, m * n : (m + 1) * n, :], vl[s, m * n : (m + 1) * n, :]
                back = dot(a_hi, l_hi[...]) + dot(a_lo, l_hi[...]) + dot(a_hi, l_lo[...])
                br, bi = back[:, :n], back[:, n:]
                pr, pi = probe_ref[k, 0], probe_ref[k, 1]
                gr, gi = pr * br + pi * bi, pr * bi - pi * br
                wr, wi = win[s, 0], win[s, 1]
                tr, ti = wr * br + wi * bi, wr * bi - wi * br
                if k == 0:
                    gacc[s, 0], gacc[s, 1] = gr, gi
                else:
                    gacc[s, 0], gacc[s, 1] = gacc[s, 0] + gr, gacc[s, 1] + gi
                if s == 0:
                    term[k, 0], term[k, 1] = tr, ti
                else:
                    term[k, 0], term[k, 1] = term[k, 0] + tr, term[k, 1] + ti
        to_partner(p).start()

    def row_slice(ref, p, owner):
        return ref.at[p, pl.ds(pl.multiple_of(owner * chunk, 8), chunk)]

    def scatter(p, hop):
        to = lax.rem(me + hop, rows)
        src = lax.rem(me + rows - hop, rows)
        return (
            to,
            remote(row_slice(acc, p, to), pieces.at[p, hop], rs_send.at[p, hop], rs_recv.at[p, hop], {"row": to}),
        )

    def start_scatter(p):
        to_partner(p).wait()
        for q in range(2):
            acc[p, q * n : (q + 1) * n] = term[2 * p + col, q] + tpart[p, q]

        def step(hop):
            to, copy = scatter(p, hop)
            pl.when(to < owners)(copy.start)

        each_peer(rows, step)

    hear(len(rounds) - 1)
    start_scatter(0)

    for q in range(2):
        own = [jnp.zeros((n, n), F32)] * 3
        par = [jnp.zeros((n, n), F32)] * 3
        for s in range(slots):
            by, bx, sy, sx = place(s)
            g = pltpu.roll(pltpu.roll(gacc[s, q], sy, 0), sx, 1)
            low_x, low_y = (lane_id >= sx).astype(F32), (row_id >= sy).astype(F32)

            def side(block, at, low):
                return (block == at).astype(F32) * low + (block == at + 1).astype(F32) * (1.0 - low)

            g_own, g_par = g * side(1, bx, low_x), g * side(mine, bx, low_x)
            for j in range(3):
                mask = side(j, by, low_y)
                own[j] = own[j] + g_own * mask
                par[j] = par[j] + g_par * mask
        for j in range(3):
            gown[j, q] = own[j]
            gpar[j, q] = par[j]
    across = remote(gpar, grecv, g_send.at[0], g_recv.at[0], mate)
    across.start()


    for p in range(1, modes // 2):
        start_scatter(p)

    across.wait()
    for j in range(3):
        gown[j] = gown[j] + grecv[j]
    edge_up = remote(gown.at[0], gedge.at[1], e_send.at[0], e_recv.at[1], up)
    edge_down = remote(gown.at[2], gedge.at[0], e_send.at[1], e_recv.at[0], down)
    pl.when(has_up)(edge_up.start)
    pl.when(has_down)(edge_down.start)

    def gather(p, hop):
        to = lax.rem(me + hop, rows)
        here = row_slice(red, p, me)
        return remote(here, here, ag_send.at[p, hop], ag_recv.at[p, hop], {"row": to})

    for p in range(modes // 2):

        @pl.when(me < owners)
        def _():
            red_chunk = row_slice(acc, p, me)[...]

            if rows <= 16:
                for hop in range(1, rows):
                    scatter(p, hop)[1].wait_recv()
                    red_chunk = red_chunk + pieces[p, hop]
            else:

                def add(hop, total):
                    scatter(p, hop)[1].wait_recv()
                    return total + pieces[p, hop]

                red_chunk = lax.fori_loop(1, rows, add, red_chunk)
            row_slice(red, p, me)[...] = red_chunk
            each_peer(rows, lambda hop: gather(p, hop).start())

    @pl.when(jnp.logical_not(has_up))
    def _():
        gedge[0] = zero

    @pl.when(jnp.logical_not(has_down))
    def _():
        gedge[1] = zero

    pl.when(has_up)(edge_down.wait_recv)
    pl.when(has_down)(edge_up.wait_recv)
    for q in range(2):
        grad = gown[1, q] + gedge[0, q] + gedge[1, q]
        obj_out[q] = object_rate * grad / weight

    def swap(p):
        return remote(red.at[p], red_other.at[p], o_send.at[p], o_recv.at[p], mate)

    for p in range(modes // 2):

        def step(hop):
            src = lax.rem(me + rows - hop, rows)
            pl.when(src < owners)(gather(p, hop).wait_recv)

        each_peer(rows, step)
        swap(p).start()
        k = 2 * p + col
        for q in range(2):
            probe_out[k, q] = probe_rate * red[p, q * n : (q + 1) * n] / tiles
    for p in range(modes // 2):
        swap(p).wait()
        k = 2 * p + 1 - col
        for q in range(2):
            probe_out[k, q] = probe_rate * red_other[p, q * n : (q + 1) * n] / tiles

    to_mate.wait_send()

    @pl.when(has_up)
    def _():
        to_up.wait_send()
        relay_up.wait_send()
        edge_up.wait_send()

    @pl.when(has_down)
    def _():
        to_down.wait_send()
        relay_down.wait_send()
        edge_down.wait_send()

    for p in range(modes // 2):

        def drain(hop):
            to, copy = scatter(p, hop)
            pl.when(to < owners)(copy.wait_send)
            pl.when(me < owners)(gather(p, hop).wait_send)

        each_peer(rows, drain)


def finish(obj_ref, probe_ref, obj_step, probe_step, obj_out, probe_out):
    obj_out[...] = obj_ref[...] - obj_step[...]
    probe_out[...] = probe_ref[...] - probe_step[...]


def body(rows, object_field, probe, patterns, offsets, counts):
    modes, _, n, _ = probe.shape
    slots = patterns.shape[2]
    pairs = modes // 2
    owners = min(rows, 2 * n // 8)
    tables = jnp.asarray(dft_tables(n))
    vmem = pl.BlockSpec(memory_space=pltpu.VMEM)
    smem = pl.BlockSpec(memory_space=pltpu.SMEM)
    dma = pltpu.SemaphoreType.DMA
    wide, tall = (slots, 2 * n, modes * n), (slots, modes * n, 2 * n)
    steps = pl.pallas_call(
        functools.partial(kernel, rows, modes, slots, n, owners),
        out_shape=(
            jax.ShapeDtypeStruct(object_field.shape, F32),
            jax.ShapeDtypeStruct(probe.shape, F32),
        ),
        in_specs=[smem, smem, vmem, vmem, vmem, vmem],
        out_specs=(vmem, vmem),
        scratch_shapes=[
            pltpu.VMEM((3, 3, 2, n, n), F32),
            pltpu.VMEM(tall, BF16),
            pltpu.VMEM(tall, BF16),
            pltpu.VMEM(wide, BF16),
            pltpu.VMEM(wide, BF16),
            pltpu.VMEM(wide, F32),
            pltpu.VMEM((slots, 2 * n, 2 * n), BF16),
            pltpu.VMEM((slots, 2 * n, 2 * n), BF16),
            pltpu.VMEM((slots, 2, n, n), F32),
            pltpu.VMEM((slots, 2, n, n), F32),
            pltpu.VMEM((3, 2, n, n), F32),
            pltpu.VMEM((3, 2, n, n), F32),
            pltpu.VMEM((3, 2, n, n), F32),
            pltpu.VMEM((2, 2, n, n), F32),
            pltpu.VMEM((modes, 2, n, n), F32),
            pltpu.VMEM((pairs, 2, n, n), F32),
            pltpu.VMEM((pairs, 2 * n, n), F32),
            pltpu.VMEM((pairs, rows, 2 * n // owners, n), F32),
            pltpu.VMEM((pairs, 2 * n, n), F32),
            pltpu.VMEM((pairs, 2 * n, n), F32),
            dma((5,)), dma((5,)), dma((1,)), dma((1,)), dma((2,)), dma((2,)),
            dma((pairs,)), dma((pairs,)),
            dma((pairs, rows)), dma((pairs, rows)), dma((pairs, rows)), dma((pairs, rows)),
            dma((pairs,)), dma((pairs,)), pltpu.SemaphoreType.REGULAR((max(1, rows.bit_length()),)),
        ],
        compiler_params=pltpu.CompilerParams(collective_id=0, has_side_effects=True),
    )(offsets, counts, object_field, probe, patterns, tables)
    return pl.pallas_call(
        finish,
        out_shape=(
            jax.ShapeDtypeStruct(object_field.shape, F32),
            jax.ShapeDtypeStruct(probe.shape, F32),
        ),
        in_specs=[vmem] * 4,
        out_specs=(vmem, vmem),
    )(object_field, probe, *steps)


def solution(mesh):
    placed = (
        P(None, ("tilt", "row"), "col"),
        P("tilt", None, None, None),
        P(("tilt", "row"), "col", None, None, None),
        P(("tilt", "row"), "col", None, None),
        P(("tilt", "row"), "col"),
    )
    return jax.shard_map(
        functools.partial(body, mesh.shape["row"]),
        mesh=mesh,
        in_specs=placed,
        out_specs=(P(None, ("tilt", "row"), "col"), P("tilt", None, None, None)),
        check_vma=False,
    )
```

profile of v0, /device:TPU:0, one launch (start us, length us, event | category | flops | bytes accessed | tf_op | source)
XLA Modules:
  0.0 39.9 jit_solution(410661510106563803)
XLA Ops:
  1.3 36.4 %shard_map.77 = (f32[2,128,128]{2,1,0:T(8,128)}, f32[4,2,128,128]{3,2,1,0:T(8,128)}) custom-call(s32[1,1,2,2]{3,2,1,0:T(2,128)} %off_ref.1, s32[1,1]{1,0:T(1,128)S(6)} %copy.8.cnt_ref, f32[2,128,128]{2,1,0:T(8,128)} %obj_ref.3, f32[4,2,128,128]{3,2,1,0:T(8,128)} %probe_ref.3, f32[1,1,2,128,128]{4,3,2,1,0:T(8,128)} %pat_ref.1, ...), custom_call_target="tpu_custom_call" | custom-call | tf_op jit(solution)/shard_map/pallas_call | solution.py:396
  37.7 2.1 %shard_map.78 = (f32[2,128,128]{2,1,0:T(8,128)}, f32[4,2,128,128]{3,2,1,0:T(8,128)}) custom-call(f32[2,128,128]{2,1,0:T(8,128)} %obj_ref.3, f32[4,2,128,128]{3,2,1,0:T(8,128)} %probe_ref.3, f32[2,128,128]{2,1,0:T(8,128)} %get-tuple-element.4.obj_step, f32[4,2,128,128]{3,2,1,0:T(8,128)} %get-tuple-element.5.probe_step), custom_call_target="tpu_custom_call" | custom-call | tf_op jit(solution)/shard_map/pallas_call | solution.py:432
where the time goes:
time: 40 us; the launch traced here: 39.9 us
  Pallas kernels  38.6 us (96%)
  between operations  1.28 us (3%)
    pallas_call x1, Pallas kernels, body(): pl.pallas_call(functools.partial(kernel, rows, modes, slots, n, owners),...  36.4 us
    pallas_call x1, Pallas kernels, body(): pl.pallas_call(finish, out_shape=(jax.ShapeDtypeStruct(object_field.shape...  2.14 us

commit v1 on v0

v1 whole, which is shorter than its diff:
```python
import contextlib
import functools

import jax
import jax.numpy as jnp
import numpy as np
from jax import lax
from jax.experimental import pallas as pl
from jax.experimental.pallas import tpu as pltpu
from jax.sharding import PartitionSpec as P

MESH = pl.DeviceIdType.MESH
F32 = jnp.float32
BF16 = jnp.bfloat16

object_rate = 1.0
probe_rate = 1.0
epsilon = 1e-06


def mark(name):
    return contextlib.nullcontext()


def split_table(table):
    high = table.astype(jnp.bfloat16)
    low = (table - high.astype(np.float64)).astype(jnp.bfloat16)
    return high, low


def dft_tables(length):
    counter = np.arange(length)
    product = counter[:, None] * counter[None, :] % length
    angle = -2.0 * np.pi / length * product
    c, s = np.cos(angle) / np.sqrt(length), np.sin(angle) / np.sqrt(length)
    right = np.block([[c, s], [-s, c]])
    left = right.T
    return np.stack([*split_table(right), *split_table(left)])


def split(x):
    high = x.astype(BF16)
    return high, (x - high.astype(F32)).astype(BF16)


def dot(a, b):
    return jnp.dot(a, b, preferred_element_type=F32)


def plan(rows):
    assert rows & (rows - 1) == 0
    group = min(4, rows)
    ways = []
    while group << len(ways) < rows:
        ways.append(group << len(ways))
    return group, ways


CUTS = 2
STRIPS = 2


def kernel(
    rows, modes, slots, width,
    off_hbm, cnt_hbm, obj_hbm, probe_hbm, pat_hbm, tab_hbm,
    obj_out, probe_out,
    off_ref, cnt_ref, probe_ref, pat_ref, tab_ref,
    frame, xh, xl, yh, yl, far, vh, vl, win, gacc,
    gown, gpar, grecv, gedge, term, tpart, acc, pieces, part, swapped, fin, fin_other,
    load, hm_send, hm_recv, h_send, h_recv, r_send, r_recv, g_send, g_recv, e_send, e_recv, t_send, t_recv,
    rs_send, rs_recv, x_send, x_recv, ag_send, ag_recv, o_send, o_recv,
):
    me = lax.axis_index("row")
    col = lax.axis_index("col")
    n = width
    tiles = rows * 2
    pairs = modes // 2
    group, ways = plan(rows)
    slab = 2 * n // group
    chunk = slab // CUTS
    mate = {"col": 1 - col}
    up = {"row": me - 1}
    down = {"row": me + 1}
    has_up, has_down = me > 0, me < rows - 1
    seat = lax.rem(me, group)

    def flip(index, bit):
        return jnp.where(lax.rem(index // bit, 2) == 0, index + bit, index - bit)

    def hop_to(index, hop):
        for b in range(hop.bit_length()):
            if hop >> b & 1:
                index = flip(index, 1 << b)
        return index

    def mode_at(spot):
        return 2 * spot + 1 - col if spot < pairs else 2 * (spot - pairs) + col

    loads = [
        pltpu.make_async_copy(obj_hbm, frame.at[1, 1], load.at[0]),
        pltpu.make_async_copy(off_hbm, off_ref, load.at[1]),
        pltpu.make_async_copy(cnt_hbm, cnt_ref, load.at[2]),
        pltpu.make_async_copy(pat_hbm, pat_ref, load.at[3]),
        pltpu.make_async_copy(tab_hbm, tab_ref, load.at[4]),
    ]
    probes = [
        pltpu.make_async_copy(probe_hbm.at[mode_at(j)], probe_ref.at[j], load.at[5 + j]) for j in range(modes)
    ]

    barrier = pltpu.get_barrier_semaphore()

    def greet(to):
        pl.semaphore_signal(barrier, inc=1, device_id=to, device_id_type=MESH)

    pl.when(has_up)(lambda: greet(up))
    pl.when(has_down)(lambda: greet(down))
    for hop in range(1, group):
        greet({"row": hop_to(me, hop)})
    for way in ways:
        greet({"row": flip(me, way)})
    greet(mate)
    for copy in loads + probes:
        copy.start()
    with mark("w_barrier"):
        pl.semaphore_wait(
            barrier, 1 + has_up.astype(jnp.int32) + has_down.astype(jnp.int32) + group - 1 + len(ways)
        )

    def remote(src, dst, send, recv, to):
        return pltpu.make_async_remote_copy(
            src_ref=src, dst_ref=dst, send_sem=send, recv_sem=recv, device_id=to, device_id_type=MESH
        )

    seen = 2 * col
    mine = 2 - 2 * col
    strip = n // STRIPS
    strips = [(q, pl.ds(h * strip, strip)) for q in range(2) for h in range(STRIPS)]
    to_mate = remote(obj_hbm, frame.at[1, seen], hm_send.at[0], hm_recv.at[0], mate)

    def halo(side, i):
        q, at = strips[i]
        return remote(
            obj_hbm.at[q, at], frame.at[2 * side, 1, q, at], h_send.at[side, i], h_recv.at[side, i], (down, up)[side]
        )

    def relay(side, i):
        q, at = strips[i]
        return remote(
            frame.at[2 * side, 1, q, at], frame.at[2 * side, seen, q, at],
            r_send.at[side, i], r_recv.at[side, i], mate,
        )

    sent = ((0, has_down), (1, has_up))
    got = ((0, has_up), (1, has_down))

    @pl.when(lax.rem(me, 2) == 0)
    def _():
        for side, has in sent[::-1]:
            for i in range(len(strips)):
                pl.when(has)(halo(side, i).start)

    @pl.when(lax.rem(me, 2) == 1)
    def _():
        for side, has in sent:
            for i in range(len(strips)):
                pl.when(has)(halo(side, i).start)

    to_mate.start()

    zero = jnp.zeros((2, n, n), F32)
    for j in range(3):
        frame[j, seen] = zero

    @pl.when(me == 0)
    def _():
        frame[0, 1] = zero
        frame[0, mine] = zero
        gedge[0] = zero

    @pl.when(me == rows - 1)
    def _():
        frame[2, 1] = zero
        frame[2, mine] = zero
        gedge[1] = zero

    with mark("w_load"):
        for copy in probes:
            copy.wait()
    power = jnp.zeros((n, n), F32)
    for k in range(modes):
        power = power + (probe_ref[k, 0] * probe_ref[k, 0] + probe_ref[k, 1] * probe_ref[k, 1])
    weight = jnp.max(power) + epsilon

    with mark("w_halo"):
        @pl.when(lax.rem(me, 2) == 0)
        def _():
            for side, has in got[::-1]:
                for i in range(len(strips)):
                    @pl.when(has)
                    def _():
                        halo(side, i).wait_recv()
                        relay(side, i).start()

        @pl.when(lax.rem(me, 2) == 1)
        def _():
            for side, has in got:
                for i in range(len(strips)):
                    @pl.when(has)
                    def _():
                        halo(side, i).wait_recv()
                        relay(side, i).start()

    for copy in loads:
        copy.wait()
    to_mate.wait_recv()
    with mark("w_relay"):
        for side, has in got:
            for i in range(len(strips)):
                pl.when(has)(relay(side, i).wait_recv)

    r_hi, r_lo, l_hi, l_lo = (tab_ref.at[t] for t in range(4))
    row_id = lax.broadcasted_iota(jnp.int32, (n, n), 0)
    lane_id = lax.broadcasted_iota(jnp.int32, (n, n), 1)

    def place(s):
        oy, ox = off_ref[0, 0, s, 0], off_ref[0, 0, s, 1]
        by, bx = oy // n, ox // n
        return by, bx, oy - by * n, ox - bx * n

    for s in range(slots):
        by, bx, sy, sx = place(s)
        by2, bx2 = jnp.minimum(by + 1, 2), jnp.minimum(bx + 1, 2)
        for q in range(2):
            upper = jnp.where(lane_id >= sx, frame[by, bx, q], frame[by, bx2, q])
            lower = jnp.where(lane_id >= sx, frame[by2, bx, q], frame[by2, bx2, q])
            packed = jnp.where(row_id >= sy, upper, lower)
            packed = pltpu.roll(packed, lax.rem(n - sy, n), 0)
            win[s, q] = pltpu.roll(packed, lax.rem(n - sx, n), 1)
        for k in range(modes):
            wr, wi = win[s, 0], win[s, 1]
            pr, pi = probe_ref[k, 0], probe_ref[k, 1]
            for q, value in enumerate((pr * wr - pi * wi, pr * wi + pi * wr)):
                hi, lo = split(value)
                xh[s, k * n : (k + 1) * n, q * n : (q + 1) * n] = hi
                xl[s, k * n : (k + 1) * n, q * n : (q + 1) * n] = lo
        for k in range(modes):
            a_hi, a_lo = xh[s, k * n : (k + 1) * n, :], xl[s, k * n : (k + 1) * n, :]
            y = dot(a_hi, r_hi[...]) + dot(a_lo, r_hi[...]) + dot(a_hi, r_lo[...])
            for q in range(2):
                hi, lo = split(y[:, q * n : (q + 1) * n])
                yh[s, q * n : (q + 1) * n, k * n : (k + 1) * n] = hi
                yl[s, q * n : (q + 1) * n, k * n : (k + 1) * n] = lo
        for p in range(modes // 2):
            cols = slice(2 * p * n, 2 * (p + 1) * n)
            b_hi, b_lo = yh[s, :, cols], yl[s, :, cols]
            far[s, :, cols] = dot(l_hi[...], b_hi) + dot(l_lo[...], b_hi) + dot(l_hi[...], b_lo)
        level = jnp.zeros((n, n), F32)
        for k in range(modes):
            cols = slice(k * n, (k + 1) * n)
            level = level + far[s, :n, cols] * far[s, :n, cols] + far[s, n:, cols] * far[s, n:, cols]
        live = (s < cnt_ref[0, 0]).astype(F32)
        misfit = live * (level - pat_ref[0, 0, s])
        for k in range(modes):
            for q in range(2):
                spot = (s, slice(q * n, (q + 1) * n), slice(k * n, (k + 1) * n))
                hi, lo = split(misfit * far[spot])
                yh[spot] = hi
                yl[spot] = lo

    def to_partner(p):
        return remote(term.at[p], tpart.at[p], t_send.at[p], t_recv.at[p], mate)

    def rows_of(owner, c):
        return pl.ds(pl.multiple_of(owner * slab + c * chunk, 8), chunk)

    def scatter(p, c, hop):
        return remote(
            acc.at[p, rows_of(hop_to(seat, hop), c)], pieces.at[hop - 1, p, pl.ds(c * chunk, chunk)],
            rs_send.at[hop - 1, p, c], rs_recv.at[hop - 1, p, c], {"row": hop_to(me, hop)},
        )

    hops = list(range(1, group))
    for b in range(modes // 2):
        cols = slice(2 * b * n, 2 * (b + 1) * n)
        for s in range(slots):
            b_hi, b_lo = yh[s, :, cols], yl[s, :, cols]
            v = dot(r_hi[...], b_hi) + dot(r_lo[...], b_hi) + dot(r_hi[...], b_lo)
            for m in range(2):
                for q in range(2):
                    hi, lo = split(v[q * n : (q + 1) * n, m * n : (m + 1) * n])
                    vh[s, m * n : (m + 1) * n, q * n : (q + 1) * n] = hi
                    vl[s, m * n : (m + 1) * n, q * n : (q + 1) * n] = lo
        for m in range(2):
            k = 2 * b + m
            for s in range(slots):
                a_hi, a_lo = vh[s, m * n : (m + 1) * n, :], vl[s, m * n : (m + 1) * n, :]
                back = dot(a_hi, l_hi[...]) + dot(a_lo, l_hi[...]) + dot(a_hi, l_lo[...])
                br, bi = back[:, :n], back[:, n:]
                pr, pi = probe_ref[k, 0], probe_ref[k, 1]
                gr, gi = pr * br + pi * bi, pr * bi - pi * br
                wr, wi = win[s, 0], win[s, 1]
                tr, ti = wr * br + wi * bi, wr * bi - wi * br
                if k == 0:
                    gacc[s, 0], gacc[s, 1] = gr, gi
                else:
                    gacc[s, 0], gacc[s, 1] = gacc[s, 0] + gr, gacc[s, 1] + gi
                if s == 0:
                    term[k, :n], term[k, n:] = tr, ti
                else:
                    term[k, :n], term[k, n:] = term[k, :n] + tr, term[k, n:] + ti
            if k < pairs:
                to_partner(k).start()
            else:
                p = k - pairs
                with mark("w_partner"):
                    to_partner(p).wait_recv()
                acc[p] = term[k] + tpart[p]
                for c in range(CUTS):
                    for hop in hops:
                        scatter(p, c, hop).start()

    def across(j):
        return remote(gpar.at[j], grecv.at[j], g_send.at[j], g_recv.at[j], mate)

    for q in range(2):
        own = [jnp.zeros((n, n), F32)] * 3
        par = [jnp.zeros((n, n), F32)] * 3
        for s in range(slots):
            by, bx, sy, sx = place(s)
            g = pltpu.roll(pltpu.roll(gacc[s, q], sy, 0), sx, 1)
            low_x, low_y = (lane_id >= sx).astype(F32), (row_id >= sy).astype(F32)

            def side_of(block, at, low):
                return (block == at).astype(F32) * low + (block == at + 1).astype(F32) * (1.0 - low)

            g_own, g_par = g * side_of(1, bx, low_x), g * side_of(mine, bx, low_x)
            for j in range(3):
                mask = side_of(j, by, low_y)
                own[j] = own[j] + g_own * mask
                par[j] = par[j] + g_par * mask
        for j in range(3):
            gown[j, q] = own[j]
            gpar[j, q] = par[j]
    for j in (0, 2, 1):
        across(j).start()

    edge_up = remote(gown.at[0], gedge.at[1], e_send.at[0], e_recv.at[1], up)
    edge_down = remote(gown.at[2], gedge.at[0], e_send.at[1], e_recv.at[0], down)
    with mark("w_across"):
        for j, has, edge in ((0, has_up, edge_up), (2, has_down, edge_down)):
            across(j).wait_recv()
            gown[j] = gown[j] + grecv[j]
            pl.when(has)(edge.start)

    chunks = [(p, c) for p in range(pairs) for c in range(CUTS)]

    def exchange(r, p, c):
        at = pl.ds(c * chunk, chunk)
        return remote(
            part.at[r, p, at], swapped.at[r, p, at], x_send.at[r, p, c], x_recv.at[r, p, c],
            {"row": flip(me, ways[r])},
        )

    def gather(p, c, hop):
        here = fin.at[p, rows_of(seat, c)]
        return remote(
            here, here, ag_send.at[hop - 1, p, c], ag_recv.at[hop - 1, p, c], {"row": hop_to(me, hop)}
        )

    def share(p, c, hop):
        at = rows_of(hop_to(seat, hop), c)
        return remote(fin.at[p, at], fin_other.at[p, at], o_send.at[hop, p, c], o_recv.at[hop, p, c], mate)

    def settle(r, p, c, total):
        if r < len(ways):
            part[r, p, c * chunk : (c + 1) * chunk] = total
            exchange(r, p, c).start()
        else:
            fin[p, rows_of(seat, c)] = total
            for hop in hops:
                gather(p, c, hop).start()
            share(p, c, 0).start()

    for p, c in chunks:
        total = acc[p, rows_of(seat, c)]
        with mark("w_rs"):
            for hop in hops:
                scatter(p, c, hop).wait_recv()
        for hop in hops:
            total = total + pieces[hop - 1, p, c * chunk : (c + 1) * chunk]
        settle(0, p, c, total)
    for r in range(len(ways)):
        for p, c in chunks:
            with mark("w_xc"):
                exchange(r, p, c).wait_recv()
            at = slice(c * chunk, (c + 1) * chunk)
            settle(r + 1, p, c, part[r, p, at] + swapped[r, p, at])

    with mark("w_edge"):
        across(1).wait_recv()
        pl.when(has_up)(edge_down.wait_recv)
        pl.when(has_down)(edge_up.wait_recv)
    for q in range(2):
        grad = gown[1, q] + grecv[1, q] + gedge[0, q] + gedge[1, q]
        obj_out[q] = frame[1, 1, q] - object_rate * grad / weight

    for p, c in chunks:
        for hop in hops:
            with mark("w_ag"):
                gather(p, c, hop).wait_recv()
            share(p, c, hop).start()
    for p in range(pairs):
        for q in range(2):
            half = slice(q * n, (q + 1) * n)
            probe_out[2 * p + col, q] = probe_ref[pairs + p, q] - probe_rate * fin[p, half] / tiles
    for p in range(pairs):
        with mark("w_share"):
            for c in range(CUTS):
                for hop in range(group):
                    share(p, c, hop).wait_recv()
        for q in range(2):
            half = slice(q * n, (q + 1) * n)
            probe_out[2 * p + 1 - col, q] = probe_ref[p, q] - probe_rate * fin_other[p, half] / tiles

    with mark("w_sends"):
        to_mate.wait_send()
        for side, has in sent:
            for i in range(len(strips)):
                pl.when(has)(halo(side, i).wait_send)
        for side, has in got:
            for i in range(len(strips)):
                pl.when(has)(relay(side, i).wait_send)
        for p in range(pairs):
            to_partner(p).wait_send()
        for j in range(3):
            across(j).wait_send()
        pl.when(has_up)(edge_up.wait_send)
        pl.when(has_down)(edge_down.wait_send)
        for p, c in chunks:
            for hop in hops:
                scatter(p, c, hop).wait_send()
                gather(p, c, hop).wait_send()
            for r in range(len(ways)):
                exchange(r, p, c).wait_send()
            for hop in range(group):
                share(p, c, hop).wait_send()


def finish(obj_ref, probe_ref, obj_out, probe_out, sem):
    copies = [pltpu.make_async_copy(obj_ref, obj_out, sem.at[0]), pltpu.make_async_copy(probe_ref, probe_out, sem.at[1])]
    for copy in copies:
        copy.start()
    for copy in copies:
        copy.wait()


def body(rows, object_field, probe, patterns, offsets, counts):
    modes, _, n, _ = probe.shape
    slots = patterns.shape[2]
    pairs = modes // 2
    group, ways = plan(rows)
    rounds = max(1, len(ways))
    far_hops = max(1, group - 1)
    slab = 2 * n // group
    tables = jnp.asarray(dft_tables(n))
    vmem = pl.BlockSpec(memory_space=pltpu.VMEM)
    hbm = pl.BlockSpec(memory_space=pltpu.HBM)
    dma = pltpu.SemaphoreType.DMA
    wide, tall = (slots, 2 * n, modes * n), (slots, modes * n, 2 * n)
    outs = (
        jax.ShapeDtypeStruct(object_field.shape, F32),
        jax.ShapeDtypeStruct(probe.shape, F32),
    )
    results = pl.pallas_call(
        functools.partial(kernel, rows, modes, slots, n),
        out_shape=outs,
        in_specs=[hbm] * 6,
        out_specs=(vmem, vmem),
        scratch_shapes=[
            pltpu.SMEM(offsets.shape, jnp.int32),
            pltpu.SMEM(counts.shape, jnp.int32),
            pltpu.VMEM(probe.shape, F32),
            pltpu.VMEM(patterns.shape, F32),
            pltpu.VMEM(tables.shape, BF16),
            pltpu.VMEM((3, 3, 2, n, n), F32),
            pltpu.VMEM(tall, BF16),
            pltpu.VMEM(tall, BF16),
            pltpu.VMEM(wide, BF16),
            pltpu.VMEM(wide, BF16),
            pltpu.VMEM(wide, F32),
            pltpu.VMEM((slots, 2 * n, 2 * n), BF16),
            pltpu.VMEM((slots, 2 * n, 2 * n), BF16),
            pltpu.VMEM((slots, 2, n, n), F32),
            pltpu.VMEM((slots, 2, n, n), F32),
            pltpu.VMEM((3, 2, n, n), F32),
            pltpu.VMEM((3, 2, n, n), F32),
            pltpu.VMEM((3, 2, n, n), F32),
            pltpu.VMEM((2, 2, n, n), F32),
            pltpu.VMEM((modes, 2 * n, n), F32),
            pltpu.VMEM((pairs, 2 * n, n), F32),
            pltpu.VMEM((pairs, 2 * n, n), F32),
            pltpu.VMEM((far_hops, pairs, slab, n), F32),
            pltpu.VMEM((rounds, pairs, slab, n), F32),
            pltpu.VMEM((rounds, pairs, slab, n), F32),
            pltpu.VMEM((pairs, 2 * n, n), F32),
            pltpu.VMEM((pairs, 2 * n, n), F32),
            dma((5 + modes,)),
            dma((1,)), dma((1,)),
            dma((2, 2 * STRIPS)), dma((2, 2 * STRIPS)),
            dma((2, 2 * STRIPS)), dma((2, 2 * STRIPS)),
            dma((3,)), dma((3,)),
            dma((2,)), dma((2,)),
            dma((pairs,)), dma((pairs,)),
            dma((far_hops, pairs, CUTS)), dma((far_hops, pairs, CUTS)),
            dma((rounds, pairs, CUTS)), dma((rounds, pairs, CUTS)),
            dma((far_hops, pairs, CUTS)), dma((far_hops, pairs, CUTS)),
            dma((group, pairs, CUTS)), dma((group, pairs, CUTS)),
        ],
        compiler_params=pltpu.CompilerParams(
            collective_id=0, has_side_effects=True, vmem_limit_bytes=24 << 20
        ),
    )(*[pltpu.with_memory_space_constraint(x, pltpu.HBM) for x in (offsets,)], counts, *[pltpu.with_memory_space_constraint(x, pltpu.HBM) for x in (object_field, probe, patterns, tables)])
    return pl.pallas_call(
        finish,
        out_shape=outs,
        in_specs=[vmem] * 2,
        out_specs=(hbm, hbm),
        scratch_shapes=[dma((2,))],
        compiler_params=pltpu.CompilerParams(vmem_limit_bytes=4 << 20),
    )(*results)


def solution(mesh):
    placed = (
        P(None, ("tilt", "row"), "col"),
        P("tilt", None, None, None),
        P(("tilt", "row"), "col", None, None, None),
        P(("tilt", "row"), "col", None, None),
        P(("tilt", "row"), "col"),
    )
    return jax.shard_map(
        functools.partial(body, mesh.shape["row"]),
        mesh=mesh,
        in_specs=placed,
        out_specs=(P(None, ("tilt", "row"), "col"), P("tilt", None, None, None)),
        check_vma=False,
    )
```

time: 40 us -> 33.7 us (0.84)
  Pallas kernels: 38.6 us -> 32.3 us
    pallas_call x2, Pallas kernels: 38.6 us -> 32.3 us  [the longest x1 31.4 us: body(): pl.pallas_call(functools.partial(kernel, rows, modes, slots, n), out_shap...]
where the time goes in v1:
time: 33.7 us; the launch traced here: 33.6 us
  Pallas kernels  32.3 us (96%)
  between operations  1.29 us (4%)
    pallas_call x1, Pallas kernels, body(): pl.pallas_call(functools.partial(kernel, rows, modes, slots, n), out_shap...  31.4 us
    pallas_call x1, Pallas kernels, body(): pl.pallas_call(finish, out_shape=outs, in_specs=[vmem] * 2, out_specs=(hb...  0.86 us

profile of v1, /device:TPU:0, one launch (start us, length us, event | category | flops | bytes accessed | tf_op | source)
XLA Modules:
  0.0 33.6 jit_solution(14415676894486328398)
XLA Ops:
  1.3 31.4 %shard_map.77 = (f32[2,128,128]{2,1,0:T(8,128)S(1)}, f32[4,2,128,128]{3,2,1,0:T(8,128)S(1)}) custom-call(s32[1,1,2,2]{3,2,1,0:T(2,128)} %off_hbm.1, s32[1,1]{1,0:T(1,128)S(6)} %copy.8.cnt_hbm, f32[2,128,128]{2,1,0:T(8,128)} %obj_hbm.1, f32[4,2,128,128]{3,2,1,0:T(8,128)} %probe_hbm.1, f32[1,1,2,128,128]{4,3,2,1,0:T(8,128)} %pat_hbm.1, ...), custom_call_target="tpu_custom_call" | custom-call | tf_op jit(solution)/shard_map/pallas_call | solution.py:474
  32.7 0.9 %shard_map.78 = (f32[2,128,128]{2,1,0:T(8,128)}, f32[4,2,128,128]{3,2,1,0:T(8,128)}) custom-call(f32[2,128,128]{2,1,0:T(8,128)S(1)} %get-tuple-element.4.obj_ref, f32[4,2,128,128]{3,2,1,0:T(8,128)S(1)} %get-tuple-element.5.probe_ref), custom_call_target="tpu_custom_call" | custom-call | tf_op jit(solution)/shard_map/pallas_call | solution.py:523

commit v2 on v1

v2 whole, which is shorter than its diff:
```python
import contextlib
import functools

import jax
import jax.numpy as jnp
import numpy as np
from jax import lax
from jax.experimental import pallas as pl
from jax.experimental.pallas import tpu as pltpu
from jax.sharding import PartitionSpec as P

MESH = pl.DeviceIdType.MESH
F32 = jnp.float32
BF16 = jnp.bfloat16

object_rate = 1.0
probe_rate = 1.0
epsilon = 1e-06


def mark(name):
    return contextlib.nullcontext()


def split_table(table):
    high = table.astype(jnp.bfloat16)
    low = (table - high.astype(np.float64)).astype(jnp.bfloat16)
    return high, low


def dft_tables(length):
    counter = np.arange(length)
    product = counter[:, None] * counter[None, :] % length
    angle = -2.0 * np.pi / length * product
    c, s = np.cos(angle) / np.sqrt(length), np.sin(angle) / np.sqrt(length)
    right = np.block([[c, s], [-s, c]])
    left = right.T
    return np.stack([*split_table(right), *split_table(left)])


def split(x):
    high = x.astype(BF16)
    return high, (x - high.astype(F32)).astype(BF16)


def dot(a, b):
    return jnp.dot(a, b, preferred_element_type=F32)


def plan(rows):
    assert rows & (rows - 1) == 0
    group = min(4, rows)
    ways = []
    while group << len(ways) < rows:
        ways.append(group << len(ways))
    return group, ways


CUTS = 2
STRIPS = (2, 2, 2, 1, 1)


def kernel(
    rows, modes, slots, width,
    off_hbm, cnt_hbm, obj_hbm, probe_hbm, pat_hbm, tab_hbm,
    obj_out, probe_out,
    off_ref, cnt_ref, probe_ref, pat_ref, tab_ref,
    frame, xh, xl, yh, yl, far, vh, vl, win, gacc,
    gown, gpar, grecv, gnear, gfar, term, tpart, acc, pieces, part, swapped, fin, fin_other,
    load, hm_send, hm_recv, n_send, n_recv, f_send, f_recv, r_send, r_recv, g_send, g_recv,
    e_send, e_recv, t_send, t_recv, rs_send, rs_recv, x_send, x_recv, ag_send, ag_recv, o_send, o_recv,
):
    me = lax.axis_index("row")
    col = lax.axis_index("col")
    n = width
    tiles = rows * 2
    pairs = modes // 2
    group, ways = plan(rows)
    slab = 2 * n // group
    chunk = slab // CUTS
    mate = {"col": 1 - col}
    odd = lax.rem(me, 2)
    near_at, far_at = 2 - 2 * odd, 2 * odd
    near, far_row = me + 1 - 2 * odd, me - 1 + 2 * odd
    has_far = jnp.logical_and(far_row >= 0, far_row < rows)
    seat = lax.rem(me, group)

    def flip(index, bit):
        return jnp.where(lax.rem(index // bit, 2) == 0, index + bit, index - bit)

    def hop_to(index, hop):
        for b in range(hop.bit_length()):
            if hop >> b & 1:
                index = flip(index, 1 << b)
        return index

    def mode_at(spot):
        return 2 * spot + 1 - col if spot < pairs else 2 * (spot - pairs) + col

    obj_load = pltpu.make_async_copy(obj_hbm, frame.at[1, 1], load.at[0])
    loads = [
        pltpu.make_async_copy(off_hbm, off_ref, load.at[1]),
        pltpu.make_async_copy(cnt_hbm, cnt_ref, load.at[2]),
        pltpu.make_async_copy(pat_hbm, pat_ref, load.at[3]),
        pltpu.make_async_copy(tab_hbm, tab_ref, load.at[4]),
    ]
    probes = [pltpu.make_async_copy(probe_hbm.at[mode_at(j)], probe_ref.at[j], load.at[5]) for j in range(modes)]
    all_probes = pltpu.make_async_copy(probe_hbm, probe_ref, load.at[5])

    barrier = pltpu.get_barrier_semaphore()

    def greet(to):
        pl.semaphore_signal(barrier, inc=1, device_id=to, device_id_type=MESH)

    peers = [hop_to(me, hop) for hop in range(1, group)] + [flip(me, way) for way in ways]
    pl.when(has_far)(lambda: greet({"row": far_row}))
    for peer in peers:
        greet({"row": peer})
    greet(mate)
    for copy in [obj_load] + probes + loads:
        copy.start()
    with mark("w_barrier"):
        pl.semaphore_wait(
            barrier, 1 + has_far.astype(jnp.int32) + len(peers)
        )

    def remote(src, dst, send, recv, to):
        return pltpu.make_async_remote_copy(
            src_ref=src, dst_ref=dst, send_sem=send, recv_sem=recv, device_id=to, device_id_type=MESH
        )

    seen = 2 * col
    mine = 2 - 2 * col
    unit = 2 * n // sum(STRIPS)
    starts = [unit * sum(STRIPS[:i]) for i in range(len(STRIPS) + 1)]
    strips = [pl.ds(starts[i], starts[i + 1] - starts[i]) for i in range(len(STRIPS))]
    to_mate = remote(obj_hbm, frame.at[1, seen], hm_send.at[0], hm_recv.at[0], mate)

    def to_near(i, at=None):
        at = strips[i] if at is None else at
        return remote(obj_hbm.at[at], frame.at[far_at, 1, at], n_send.at[0], n_recv.at[i], {"row": near})

    def to_far(i, at=None):
        at = strips[i] if at is None else at
        return remote(obj_hbm.at[at], frame.at[near_at, 1, at], f_send.at[0], f_recv.at[i], {"row": far_row})

    def relay(block, kind, at):
        return remote(
            frame.at[block, 1, at], frame.at[block, seen, at], r_send.at[kind], r_recv.at[kind], mate
        )

    whole = pl.ds(0, 2 * n)
    last = len(STRIPS)
    for i in range(last):
        pl.when(has_far)(to_far(i).start)
        to_near(i).start()
    to_mate.start()

    zero = jnp.zeros((2 * n, n), F32)
    for j in range(3):
        frame[j, seen] = zero

    @pl.when(jnp.logical_not(has_far))
    def _():
        frame[far_at, 1] = zero
        frame[far_at, mine] = zero
        gfar[...] = zero

    with mark("w_load"):
        all_probes.wait()
    power = jnp.zeros((n, n), F32)
    for k in range(modes):
        power = power + (probe_ref[k, 0] * probe_ref[k, 0] + probe_ref[k, 1] * probe_ref[k, 1])
    weight = jnp.max(power) + epsilon

    with mark("w_halo"):
        def far_strip(i):
            @pl.when(has_far)
            def _():
                to_far(i).wait_recv()
                relay(far_at, 1, strips[i]).start()

        def near_strip(i):
            to_near(i).wait_recv()
            relay(near_at, 0, strips[i]).start()

        for i in range(last):
            near_strip(i)
            far_strip(i)

    obj_load.wait()
    for copy in loads:
        copy.wait()
    to_mate.wait_recv()
    with mark("w_relay"):
        relay(near_at, 0, whole).wait_recv()
        pl.when(has_far)(relay(far_at, 1, whole).wait_recv)

    r_hi, r_lo, l_hi, l_lo = (tab_ref.at[t] for t in range(4))
    row_id = lax.broadcasted_iota(jnp.int32, (n, n), 0)
    lane_id = lax.broadcasted_iota(jnp.int32, (n, n), 1)

    def place(s):
        oy, ox = off_ref[0, 0, s, 0], off_ref[0, 0, s, 1]
        by, bx = oy // n, ox // n
        return by, bx, oy - by * n, ox - bx * n

    for s in range(slots):
        by, bx, sy, sx = place(s)
        by2, bx2 = jnp.minimum(by + 1, 2), jnp.minimum(bx + 1, 2)
        for q in range(2):
            half = slice(q * n, (q + 1) * n)
            upper = jnp.where(lane_id >= sx, frame[by, bx, half], frame[by, bx2, half])
            lower = jnp.where(lane_id >= sx, frame[by2, bx, half], frame[by2, bx2, half])
            packed = jnp.where(row_id >= sy, upper, lower)
            packed = pltpu.roll(packed, lax.rem(n - sy, n), 0)
            win[s, q] = pltpu.roll(packed, lax.rem(n - sx, n), 1)
        for k in range(modes):
            wr, wi = win[s, 0], win[s, 1]
            pr, pi = probe_ref[k, 0], probe_ref[k, 1]
            for q, value in enumerate((pr * wr - pi * wi, pr * wi + pi * wr)):
                hi, lo = split(value)
                xh[s, k * n : (k + 1) * n, q * n : (q + 1) * n] = hi
                xl[s, k * n : (k + 1) * n, q * n : (q + 1) * n] = lo
        for k in range(modes):
            a_hi, a_lo = xh[s, k * n : (k + 1) * n, :], xl[s, k * n : (k + 1) * n, :]
            y = dot(a_hi, r_hi[...]) + dot(a_lo, r_hi[...]) + dot(a_hi, r_lo[...])
            for q in range(2):
                hi, lo = split(y[:, q * n : (q + 1) * n])
                yh[s, q * n : (q + 1) * n, k * n : (k + 1) * n] = hi
                yl[s, q * n : (q + 1) * n, k * n : (k + 1) * n] = lo
        for p in range(modes // 2):
            cols = slice(2 * p * n, 2 * (p + 1) * n)
            b_hi, b_lo = yh[s, :, cols], yl[s, :, cols]
            far[s, :, cols] = dot(l_hi[...], b_hi) + dot(l_lo[...], b_hi) + dot(l_hi[...], b_lo)
        level = jnp.zeros((n, n), F32)
        for k in range(modes):
            cols = slice(k * n, (k + 1) * n)
            level = level + far[s, :n, cols] * far[s, :n, cols] + far[s, n:, cols] * far[s, n:, cols]
        live = (s < cnt_ref[0, 0]).astype(F32)
        misfit = live * (level - pat_ref[0, 0, s])
        for k in range(modes):
            for q in range(2):
                spot = (s, slice(q * n, (q + 1) * n), slice(k * n, (k + 1) * n))
                hi, lo = split(misfit * far[spot])
                yh[spot] = hi
                yl[spot] = lo

    def to_partner(p):
        return remote(term.at[p], tpart.at[p], t_send.at[0], t_recv.at[p], mate)

    def rows_of(owner, c):
        return pl.ds(pl.multiple_of(owner * slab + c * chunk, 8), chunk)

    def scatter(p, c, hop):
        return remote(
            acc.at[p, rows_of(hop_to(seat, hop), c)], pieces.at[p, c, hop - 1],
            rs_send.at[0], rs_recv.at[p, c], {"row": hop_to(me, hop)},
        )

    hops = list(range(1, group))
    for b in range(modes // 2):
        cols = slice(2 * b * n, 2 * (b + 1) * n)
        for s in range(slots):
            b_hi, b_lo = yh[s, :, cols], yl[s, :, cols]
            v = dot(r_hi[...], b_hi) + dot(r_lo[...], b_hi) + dot(r_hi[...], b_lo)
            for m in range(2):
                for q in range(2):
                    hi, lo = split(v[q * n : (q + 1) * n, m * n : (m + 1) * n])
                    vh[s, m * n : (m + 1) * n, q * n : (q + 1) * n] = hi
                    vl[s, m * n : (m + 1) * n, q * n : (q + 1) * n] = lo
        for m in range(2):
            k = 2 * b + m
            for s in range(slots):
                a_hi, a_lo = vh[s, m * n : (m + 1) * n, :], vl[s, m * n : (m + 1) * n, :]
                back = dot(a_hi, l_hi[...]) + dot(a_lo, l_hi[...]) + dot(a_hi, l_lo[...])
                br, bi = back[:, :n], back[:, n:]
                pr, pi = probe_ref[k, 0], probe_ref[k, 1]
                gr, gi = pr * br + pi * bi, pr * bi - pi * br
                wr, wi = win[s, 0], win[s, 1]
                tr, ti = wr * br + wi * bi, wr * bi - wi * br
                if k == 0:
                    gacc[s, 0], gacc[s, 1] = gr, gi
                else:
                    gacc[s, 0], gacc[s, 1] = gacc[s, 0] + gr, gacc[s, 1] + gi
                if s == 0:
                    term[k, :n], term[k, n:] = tr, ti
                else:
                    term[k, :n], term[k, n:] = term[k, :n] + tr, term[k, n:] + ti
            if k < pairs:
                to_partner(k).start()
            else:
                p = k - pairs
                with mark("w_partner"):
                    to_partner(p).wait_recv()
                acc[p] = term[k] + tpart[p]
                for c in range(CUTS):
                    for hop in hops:
                        scatter(p, c, hop).start()

    def across(j):
        return remote(gpar.at[j], grecv.at[j], g_send.at[0], g_recv.at[j], mate)

    for q in range(2):
        own = [jnp.zeros((n, n), F32)] * 3
        par = [jnp.zeros((n, n), F32)] * 3
        for s in range(slots):
            by, bx, sy, sx = place(s)
            g = pltpu.roll(pltpu.roll(gacc[s, q], sy, 0), sx, 1)
            low_x, low_y = (lane_id >= sx).astype(F32), (row_id >= sy).astype(F32)

            def side_of(block, at, low):
                return (block == at).astype(F32) * low + (block == at + 1).astype(F32) * (1.0 - low)

            g_own, g_par = g * side_of(1, bx, low_x), g * side_of(mine, bx, low_x)
            for j in range(3):
                mask = side_of(j, by, low_y)
                own[j] = own[j] + g_own * mask
                par[j] = par[j] + g_par * mask
        for j in range(3):
            gown[j, q * n : (q + 1) * n] = own[j]
            gpar[j, q * n : (q + 1) * n] = par[j]
    edge_far = remote(gown.at[far_at], gfar, e_send.at[0], e_recv.at[0], {"row": far_row})
    edge_near = remote(gown.at[near_at], gnear, e_send.at[1], e_recv.at[1], {"row": near})
    for j in (far_at, near_at, 1):
        across(j).start()
    with mark("w_across"):
        for j in (far_at, near_at):
            across(j).wait_recv()
            gown[j] = gown[j] + grecv[j]

    chunks = [(p, c) for p in range(pairs) for c in range(CUTS)]

    def exchange(r, p, c):
        return remote(
            part.at[p, c, r], swapped.at[p, c, r], x_send.at[0], x_recv.at[p, c, r], {"row": flip(me, ways[r])}
        )

    def gather(p, c, hop):
        here = fin.at[p, rows_of(seat, c)]
        return remote(here, here, ag_send.at[0], ag_recv.at[p, c], {"row": hop_to(me, hop)})

    def share(p, c, hop):
        at = rows_of(hop_to(seat, hop), c)
        return remote(fin.at[p, at], fin_other.at[p, at], o_send.at[0], o_recv.at[p], mate)

    def settle(r, p, c, total):
        if r < len(ways):
            part[p, c, r] = total
            exchange(r, p, c).start()
        else:
            fin[p, rows_of(seat, c)] = total
            for hop in hops:
                gather(p, c, hop).start()
            share(p, c, 0).start()

    def all_of(ref, send, recv):
        return remote(ref, ref, send, recv, mate)

    for p, c in chunks:
        total = acc[p, rows_of(seat, c)]
        with mark("w_rs"):
            all_of(pieces.at[p, c], rs_send.at[0], rs_recv.at[p, c]).wait_recv()
        for hop in hops:
            total = total + pieces[p, c, hop - 1]
        settle(0, p, c, total)
        if (p, c) == chunks[0]:
            edge_near.start()
    pl.when(has_far)(edge_far.start)
    for r in range(len(ways)):
        for p, c in chunks:
            with mark("w_xc"):
                exchange(r, p, c).wait_recv()
            settle(r + 1, p, c, part[p, c, r] + swapped[p, c, r])

    for p, c in chunks:
        with mark("w_ag"):
            all_of(pieces.at[p, c], ag_send.at[0], ag_recv.at[p, c]).wait_recv()
        for hop in hops:
            share(p, c, hop).start()
    for p in range(pairs):
        for q in range(2):
            half = slice(q * n, (q + 1) * n)
            probe_out[2 * p + col, q] = probe_ref[pairs + p, q] - probe_rate * fin[p, half] / tiles
    with mark("w_edge"):
        across(1).wait_recv()
        edge_near.wait_recv()
        pl.when(has_far)(edge_far.wait_recv)
    for q in range(2):
        half = slice(q * n, (q + 1) * n)
        grad = gown[1, half] + grecv[1, half] + gnear[half] + gfar[half]
        obj_out[half] = frame[1, 1, half] - object_rate * grad / weight

    for p in range(pairs):
        with mark("w_share"):
            all_of(fin_other.at[p], o_send.at[0], o_recv.at[p]).wait_recv()
        for q in range(2):
            half = slice(q * n, (q + 1) * n)
            probe_out[2 * p + 1 - col, q] = probe_ref[p, q] - probe_rate * fin_other[p, half] / tiles

    with mark("w_sends"):
        to_mate.wait_send()
        to_near(0, whole).wait_send()
        pl.when(has_far)(to_far(0, whole).wait_send)
        relay(near_at, 0, whole).wait_send()
        pl.when(has_far)(relay(far_at, 1, whole).wait_send)
        pl.when(has_far)(edge_far.wait_send)
        edge_near.wait_send()
        for ref, send, recv in (
            (tpart, t_send, t_recv.at[0]), (gpar, g_send, g_recv.at[0]), (pieces, rs_send, rs_recv.at[0, 0]),
            (pieces, ag_send, ag_recv.at[0, 0]), (fin_other, o_send, o_recv.at[0]),
        ):
            all_of(ref, send.at[0], recv).wait_send()
        if ways:
            all_of(part, x_send.at[0], x_recv.at[0, 0, 0]).wait_send()


def finish(obj_ref, probe_ref, obj_out, probe_out, sem):
    copies = [pltpu.make_async_copy(obj_ref, obj_out, sem.at[0])]
    for k in range(probe_ref.shape[0]):
        copies.append(pltpu.make_async_copy(probe_ref.at[k], probe_out.at[k], sem.at[k + 1]))
    for copy in copies:
        copy.start()
    for copy in copies:
        copy.wait()


def body(rows, object_field, probe, patterns, offsets, counts):
    modes, _, n, _ = probe.shape
    slots = patterns.shape[2]
    pairs = modes // 2
    assert rows > 1
    group, ways = plan(rows)
    block = object_field.reshape(2 * n, n)
    rounds = max(1, len(ways))
    chunk = 2 * n // group // CUTS
    tables = jnp.asarray(dft_tables(n))
    vmem = pl.BlockSpec(memory_space=pltpu.VMEM)
    hbm = pl.BlockSpec(memory_space=pltpu.HBM)
    dma = pltpu.SemaphoreType.DMA
    wide, tall = (slots, 2 * n, modes * n), (slots, modes * n, 2 * n)
    outs = (
        jax.ShapeDtypeStruct(block.shape, F32),
        jax.ShapeDtypeStruct(probe.shape, F32),
    )
    results = pl.pallas_call(
        functools.partial(kernel, rows, modes, slots, n),
        out_shape=outs,
        in_specs=[hbm] * 6,
        out_specs=(vmem, vmem),
        scratch_shapes=[
            pltpu.SMEM(offsets.shape, jnp.int32),
            pltpu.SMEM(counts.shape, jnp.int32),
            pltpu.VMEM(probe.shape, F32),
            pltpu.VMEM(patterns.shape, F32),
            pltpu.VMEM(tables.shape, BF16),
            pltpu.VMEM((3, 3, 2 * n, n), F32),
            pltpu.VMEM(tall, BF16),
            pltpu.VMEM(tall, BF16),
            pltpu.VMEM(wide, BF16),
            pltpu.VMEM(wide, BF16),
            pltpu.VMEM(wide, F32),
            pltpu.VMEM((slots, 2 * n, 2 * n), BF16),
            pltpu.VMEM((slots, 2 * n, 2 * n), BF16),
            pltpu.VMEM((slots, 2, n, n), F32),
            pltpu.VMEM((slots, 2, n, n), F32),
            pltpu.VMEM((3, 2 * n, n), F32),
            pltpu.VMEM((3, 2 * n, n), F32),
            pltpu.VMEM((3, 2 * n, n), F32),
            pltpu.VMEM((2 * n, n), F32),
            pltpu.VMEM((2 * n, n), F32),
            pltpu.VMEM((modes, 2 * n, n), F32),
            pltpu.VMEM((pairs, 2 * n, n), F32),
            pltpu.VMEM((pairs, 2 * n, n), F32),
            pltpu.VMEM((pairs, CUTS, group - 1, chunk, n), F32),
            pltpu.VMEM((pairs, CUTS, rounds, chunk, n), F32),
            pltpu.VMEM((pairs, CUTS, rounds, chunk, n), F32),
            pltpu.VMEM((pairs, 2 * n, n), F32),
            pltpu.VMEM((pairs, 2 * n, n), F32),
            dma((6,)),
            dma((1,)), dma((1,)),
            dma((1,)), dma((len(STRIPS),)),
            dma((1,)), dma((len(STRIPS),)),
            dma((2,)), dma((2,)),
            dma((1,)), dma((3,)),
            dma((2,)), dma((2,)),
            dma((1,)), dma((pairs,)),
            dma((1,)), dma((pairs, CUTS)),
            dma((1,)), dma((pairs, CUTS, rounds)),
            dma((1,)), dma((pairs, CUTS)),
            dma((1,)), dma((pairs,)),
        ],
        compiler_params=pltpu.CompilerParams(
            collective_id=0, has_side_effects=True, vmem_limit_bytes=24 << 20
        ),
    )(*[pltpu.with_memory_space_constraint(x, pltpu.HBM) for x in (offsets,)], counts, *[pltpu.with_memory_space_constraint(x, pltpu.HBM) for x in (block, probe, patterns, tables)])
    new_block, new_probe = pl.pallas_call(
        finish,
        out_shape=outs,
        in_specs=[vmem] * 2,
        out_specs=(hbm, hbm),
        scratch_shapes=[dma((1 + modes,))],
        compiler_params=pltpu.CompilerParams(vmem_limit_bytes=4 << 20),
    )(*results)
    return new_block.reshape(object_field.shape), new_probe


def solution(mesh):
    placed = (
        P(None, ("tilt", "row"), "col"),
        P("tilt", None, None, None),
        P(("tilt", "row"), "col", None, None, None),
        P(("tilt", "row"), "col", None, None),
        P(("tilt", "row"), "col"),
    )
    return jax.shard_map(
        functools.partial(body, mesh.shape["row"]),
        mesh=mesh,
        in_specs=placed,
        out_specs=(P(None, ("tilt", "row"), "col"), P("tilt", None, None, None)),
        check_vma=False,
    )
```

time: 33.7 us -> 32.5 us (0.964)
  Pallas kernels: 32.3 us -> 31.1 us
    pallas_call x1, Pallas kernels: 31.4 us -> 30.2 us  [body(): pl.pallas_call(functools.partial(kernel, rows, modes, slots, n), out_shap...]
where the time goes in v2:
time: 32.5 us; the launch traced here: 32.4 us
  Pallas kernels  31.1 us (96%)
  between operations  1.29 us (4%)
    pallas_call x1, Pallas kernels, body(): pl.pallas_call(functools.partial(kernel, rows, modes, slots, n), out_shap...  30.2 us
    pallas_call x1, Pallas kernels, body(): pl.pallas_call(finish, out_shape=outs, in_specs=[vmem] * 2, out_specs=(hb...  0.87 us

profile of v2, /device:TPU:0, one launch (start us, length us, event | category | flops | bytes accessed | tf_op | source)
XLA Modules:
  0.0 32.4 jit_solution(11971299042067114808)
XLA Ops:
  1.3 30.2 %shard_map.77 = (f32[256,128]{1,0:T(8,128)S(1)}, f32[4,2,128,128]{3,2,1,0:T(8,128)S(1)}) custom-call(s32[1,1,2,2]{3,2,1,0:T(2,128)} %off_hbm.1, s32[1,1]{1,0:T(1,128)S(6)} %copy.8.cnt_hbm, f32[256,128]{1,0:T(8,128)} %bitcast.2, f32[4,2,128,128]{3,2,1,0:T(8,128)} %probe_hbm.1, f32[1,1,2,128,128]{4,3,2,1,0:T(8,128)} %pat_hbm.1, ...), custom_call_target="tpu_custom_call" | custom-call | tf_op jit(solution)/shard_map/pallas_call | solution.py:446
  31.5 0.9 %shard_map.78 = (f32[256,128]{1,0:T(8,128)}, f32[4,2,128,128]{3,2,1,0:T(8,128)}) custom-call(f32[256,128]{1,0:T(8,128)S(1)} %get-tuple-element.6.obj_ref, f32[4,2,128,128]{3,2,1,0:T(8,128)S(1)} %get-tuple-element.7.probe_ref), custom_call_target="tpu_custom_call" | custom-call | tf_op jit(solution)/shard_map/pallas_call | solution.py:497

commit v3 on v2

--- a/solution.py
+++ b/solution.py
@@ -47,6 +47,18 @@
     return jnp.dot(a, b, preferred_element_type=F32)
 
 
+def right3(a_hi, a_lo, hi, lo):
+    m = a_hi.shape[0]
+    both = dot(jnp.concatenate([a_hi, a_lo], 0), hi)
+    return both[:m] + both[m:] + dot(a_hi, lo)
+
+
+def left3(hi, lo, b_hi, b_lo):
+    m = hi.shape[0]
+    both = dot(jnp.concatenate([hi, lo], 0), b_hi)
+    return both[:m] + both[m:] + dot(hi, b_lo)
+
+
 def plan(rows):
     assert rows & (rows - 1) == 0
     group = min(4, rows)
@@ -66,8 +78,8 @@
     obj_out, probe_out,
     off_ref, cnt_ref, probe_ref, pat_ref, tab_ref,
     frame, xh, xl, yh, yl, far, vh, vl, win, gacc,
-    gown, gpar, grecv, gnear, gfar, term, tpart, acc, pieces, part, swapped, fin, fin_other,
-    load, hm_send, hm_recv, n_send, n_recv, f_send, f_recv, r_send, r_recv, g_send, g_recv,
+    gown, gpar, grecv, gnear, gfar, gvia, term, tpart, acc, pieces, part, swapped, fin, fin_other,
+    load, hm_send, hm_recv, n_send, n_recv, f_send, f_recv, p_send, r_send, r_recv, g_send, g_recv,
     e_send, e_recv, t_send, t_recv, rs_send, rs_recv, x_send, x_recv, ag_send, ag_recv, o_send, o_recv,
 ):
     me = lax.axis_index("row")
@@ -81,8 +93,11 @@
     mate = {"col": 1 - col}
     odd = lax.rem(me, 2)
     near_at, far_at = 2 - 2 * odd, 2 * odd
-    near, far_row = me + 1 - 2 * odd, me - 1 + 2 * odd
+    near, far_row, beyond, behind = me + 1 - 2 * odd, me - 1 + 2 * odd, me - 2 + 4 * odd, me + 2 - 4 * odd
     has_far = jnp.logical_and(far_row >= 0, far_row < rows)
+    direct = jnp.logical_and(has_far, col == 0)
+    passes = jnp.logical_and(jnp.logical_and(behind >= 0, behind < rows), col == 1)
+    passed = jnp.logical_and(has_far, col == 1)
     seat = lax.rem(me, group)
 
     def flip(index, bit):
@@ -114,6 +129,8 @@
 
     peers = [hop_to(me, hop) for hop in range(1, group)] + [flip(me, way) for way in ways]
     pl.when(has_far)(lambda: greet({"row": far_row}))
+    pl.when(passed)(lambda: greet({"row": beyond}))
+    pl.when(passes)(lambda: greet({"row": behind}))
     for peer in peers:
         greet({"row": peer})
     greet(mate)
@@ -121,7 +138,7 @@
         copy.start()
     with mark("w_barrier"):
         pl.semaphore_wait(
-            barrier, 1 + has_far.astype(jnp.int32) + len(peers)
+            barrier, 1 + has_far.astype(jnp.int32) + passed.astype(jnp.int32) + passes.astype(jnp.int32) + len(peers)
         )
 
     def remote(src, dst, send, recv, to):
@@ -144,6 +161,12 @@
         at = strips[i] if at is None else at
         return remote(obj_hbm.at[at], frame.at[near_at, 1, at], f_send.at[0], f_recv.at[i], {"row": far_row})
 
+    def pass_on(i, at=None):
+        at = strips[i] if at is None else at
+        return remote(
+            frame.at[near_at, 1, at], frame.at[far_at, 1, at], p_send.at[0], f_recv.at[i], {"row": behind}
+        )
+
     def relay(block, kind, at):
         return remote(
             frame.at[block, 1, at], frame.at[block, seen, at], r_send.at[kind], r_recv.at[kind], mate
@@ -152,8 +175,9 @@
     whole = pl.ds(0, 2 * n)
     last = len(STRIPS)
     for i in range(last):
-        pl.when(has_far)(to_far(i).start)
         to_near(i).start()
+    for i in range(last):
+        pl.when(direct)(to_far(i).start)
     to_mate.start()
 
     zero = jnp.zeros((2 * n, n), F32)
@@ -164,6 +188,9 @@
     def _():
         frame[far_at, 1] = zero
         frame[far_at, mine] = zero
+
+    @pl.when(jnp.logical_not(direct))
+    def _():
         gfar[...] = zero
 
     with mark("w_load"):
@@ -182,10 +209,12 @@
 
         def near_strip(i):
             to_near(i).wait_recv()
+            pl.when(passes)(pass_on(i).start)
             relay(near_at, 0, strips[i]).start()
 
         for i in range(last):
             near_strip(i)
+        for i in range(last):
             far_strip(i)
 
     obj_load.wait()
@@ -215,6 +244,7 @@
             packed = jnp.where(row_id >= sy, upper, lower)
             packed = pltpu.roll(packed, lax.rem(n - sy, n), 0)
             win[s, q] = pltpu.roll(packed, lax.rem(n - sx, n), 1)
+    for s in range(slots):
         for k in range(modes):
             wr, wi = win[s, 0], win[s, 1]
             pr, pi = probe_ref[k, 0], probe_ref[k, 1]
@@ -222,17 +252,20 @@
                 hi, lo = split(value)
                 xh[s, k * n : (k + 1) * n, q * n : (q + 1) * n] = hi
                 xl[s, k * n : (k + 1) * n, q * n : (q + 1) * n] = lo
+    for s in range(slots):
         for k in range(modes):
             a_hi, a_lo = xh[s, k * n : (k + 1) * n, :], xl[s, k * n : (k + 1) * n, :]
-            y = dot(a_hi, r_hi[...]) + dot(a_lo, r_hi[...]) + dot(a_hi, r_lo[...])
+            y = right3(a_hi, a_lo, r_hi[...], r_lo[...])
             for q in range(2):
                 hi, lo = split(y[:, q * n : (q + 1) * n])
                 yh[s, q * n : (q + 1) * n, k * n : (k + 1) * n] = hi
                 yl[s, q * n : (q + 1) * n, k * n : (k + 1) * n] = lo
+    for s in range(slots):
         for p in range(modes // 2):
             cols = slice(2 * p * n, 2 * (p + 1) * n)
             b_hi, b_lo = yh[s, :, cols], yl[s, :, cols]
-            far[s, :, cols] = dot(l_hi[...], b_hi) + dot(l_lo[...], b_hi) + dot(l_hi[...], b_lo)
+            far[s, :, cols] = left3(l_hi[...], l_lo[...], b_hi, b_lo)
+    for s in range(slots):
         level = jnp.zeros((n, n), F32)
         for k in range(modes):
             cols = slice(k * n, (k + 1) * n)
@@ -263,7 +296,7 @@
         cols = slice(2 * b * n, 2 * (b + 1) * n)
         for s in range(slots):
             b_hi, b_lo = yh[s, :, cols], yl[s, :, cols]
-            v = dot(r_hi[...], b_hi) + dot(r_lo[...], b_hi) + dot(r_hi[...], b_lo)
+            v = left3(r_hi[...], r_lo[...], b_hi, b_lo)
             for m in range(2):
                 for q in range(2):
                     hi, lo = split(v[q * n : (q + 1) * n, m * n : (m + 1) * n])
@@ -273,7 +306,7 @@
             k = 2 * b + m
             for s in range(slots):
                 a_hi, a_lo = vh[s, m * n : (m + 1) * n, :], vl[s, m * n : (m + 1) * n, :]
-                back = dot(a_hi, l_hi[...]) + dot(a_lo, l_hi[...]) + dot(a_hi, l_lo[...])
+                back = right3(a_hi, a_lo, l_hi[...], l_lo[...])
                 br, bi = back[:, :n], back[:, n:]
                 pr, pi = probe_ref[k, 0], probe_ref[k, 1]
                 gr, gi = pr * br + pi * bi, pr * bi - pi * br
@@ -321,6 +354,7 @@
             gown[j, q * n : (q + 1) * n] = own[j]
             gpar[j, q * n : (q + 1) * n] = par[j]
     edge_far = remote(gown.at[far_at], gfar, e_send.at[0], e_recv.at[0], {"row": far_row})
+    edge_via = remote(gown.at[far_at], gvia, e_send.at[0], e_recv.at[2], {"row": beyond})
     edge_near = remote(gown.at[near_at], gnear, e_send.at[1], e_recv.at[1], {"row": near})
     for j in (far_at, near_at, 1):
         across(j).start()
@@ -328,6 +362,7 @@
         for j in (far_at, near_at):
             across(j).wait_recv()
             gown[j] = gown[j] + grecv[j]
+        pl.when(passed)(edge_via.start)
 
     chunks = [(p, c) for p in range(pairs) for c in range(CUTS)]
 
@@ -365,8 +400,17 @@
             total = total + pieces[p, c, hop - 1]
         settle(0, p, c, total)
         if (p, c) == chunks[0]:
-            edge_near.start()
-    pl.when(has_far)(edge_far.start)
+            pl.when(col == 0)(edge_near.start)
+    pl.when(direct)(edge_far.start)
+
+    with mark("w_via"):
+
+        @pl.when(passes)
+        def _():
+            edge_via.wait_recv()
+            gown[near_at] = gown[near_at] + gvia[...]
+
+        pl.when(col == 1)(edge_near.start)
     for r in range(len(ways)):
         for p, c in chunks:
             with mark("w_xc"):
@@ -385,7 +429,7 @@
     with mark("w_edge"):
         across(1).wait_recv()
         edge_near.wait_recv()
-        pl.when(has_far)(edge_far.wait_recv)
+        pl.when(direct)(edge_far.wait_recv)
     for q in range(2):
         half = slice(q * n, (q + 1) * n)
         grad = gown[1, half] + grecv[1, half] + gnear[half] + gfar[half]
@@ -401,7 +445,8 @@
     with mark("w_sends"):
         to_mate.wait_send()
         to_near(0, whole).wait_send()
-        pl.when(has_far)(to_far(0, whole).wait_send)
+        pl.when(direct)(to_far(0, whole).wait_send)
+        pl.when(passes)(pass_on(0, whole).wait_send)
         relay(near_at, 0, whole).wait_send()
         pl.when(has_far)(relay(far_at, 1, whole).wait_send)
         pl.when(has_far)(edge_far.wait_send)
@@ -469,6 +514,7 @@
             pltpu.VMEM((3, 2 * n, n), F32),
             pltpu.VMEM((2 * n, n), F32),
             pltpu.VMEM((2 * n, n), F32),
+            pltpu.VMEM((2 * n, n), F32),
             pltpu.VMEM((modes, 2 * n, n), F32),
             pltpu.VMEM((pairs, 2 * n, n), F32),
             pltpu.VMEM((pairs, 2 * n, n), F32),
@@ -480,10 +526,10 @@
             dma((6,)),
             dma((1,)), dma((1,)),
             dma((1,)), dma((len(STRIPS),)),
-            dma((1,)), dma((len(STRIPS),)),
+            dma((1,)), dma((len(STRIPS),)), dma((1,)),
             dma((2,)), dma((2,)),
             dma((1,)), dma((3,)),
-            dma((2,)), dma((2,)),
+            dma((2,)), dma((3,)),
             dma((1,)), dma((pairs,)),
             dma((1,)), dma((pairs, CUTS)),
             dma((1,)), dma((pairs, CUTS, rounds)),

time: 32.5 us -> 31.3 us (0.963)
  Pallas kernels: 31.1 us -> 29.8 us
    pallas_call x1, Pallas kernels: 30.2 us -> 29 us  [body(): pl.pallas_call(functools.partial(kernel, rows, modes, slots, n), out_shap...]
where the time goes in v3:
time: 31.3 us; the launch traced here: 31.1 us
  Pallas kernels  29.8 us (95%)
  between operations  1.29 us (4%)
    pallas_call x1, Pallas kernels, body(): pl.pallas_call(functools.partial(kernel, rows, modes, slots, n), out_shap...  29 us
    pallas_call x1, Pallas kernels, body(): pl.pallas_call(finish, out_shape=outs, in_specs=[vmem] * 2, out_specs=(hb...  0.87 us

profile of v3, /device:TPU:0, one launch (start us, length us, event | category | flops | bytes accessed | tf_op | source)
XLA Modules:
  0.0 31.1 jit_solution(10698244322699947655)
XLA Ops:
  1.3 29.0 %shard_map.77 = (f32[256,128]{1,0:T(8,128)S(1)}, f32[4,2,128,128]{3,2,1,0:T(8,128)S(1)}) custom-call(s32[1,1,2,2]{3,2,1,0:T(2,128)} %off_hbm.1, s32[1,1]{1,0:T(1,128)S(6)} %copy.8.cnt_hbm, f32[256,128]{1,0:T(8,128)} %bitcast.2, f32[4,2,128,128]{3,2,1,0:T(8,128)} %probe_hbm.1, f32[1,1,2,128,128]{4,3,2,1,0:T(8,128)} %pat_hbm.1, ...), custom_call_target="tpu_custom_call" | custom-call | tf_op jit(solution)/shard_map/pallas_call | solution.py:491
  30.2 0.9 %shard_map.78 = (f32[256,128]{1,0:T(8,128)}, f32[4,2,128,128]{3,2,1,0:T(8,128)}) custom-call(f32[256,128]{1,0:T(8,128)S(1)} %get-tuple-element.6.obj_ref, f32[4,2,128,128]{3,2,1,0:T(8,128)S(1)} %get-tuple-element.7.probe_ref), custom_call_target="tpu_custom_call" | custom-call | tf_op jit(solution)/shard_map/pallas_call | solution.py:543

commit v4 on v3

--- a/solution.py
+++ b/solution.py
@@ -80,7 +80,7 @@
     frame, xh, xl, yh, yl, far, vh, vl, win, gacc,
     gown, gpar, grecv, gnear, gfar, gvia, term, tpart, acc, pieces, part, swapped, fin, fin_other,
     load, hm_send, hm_recv, n_send, n_recv, f_send, f_recv, p_send, r_send, r_recv, g_send, g_recv,
-    e_send, e_recv, t_send, t_recv, rs_send, rs_recv, x_send, x_recv, ag_send, ag_recv, o_send, o_recv,
+    e_send, e_recv, t_send, t_recv, rs_send, rs_recv, x_send, x_recv, ag_send, ag_recv, o_send, o_recv, news,
 ):
     me = lax.axis_index("row")
     col = lax.axis_index("col")
@@ -127,19 +127,31 @@
     def greet(to):
         pl.semaphore_signal(barrier, inc=1, device_id=to, device_id_type=MESH)
 
-    peers = [hop_to(me, hop) for hop in range(1, group)] + [flip(me, way) for way in ways]
     pl.when(has_far)(lambda: greet({"row": far_row}))
-    pl.when(passed)(lambda: greet({"row": beyond}))
-    pl.when(passes)(lambda: greet({"row": behind}))
-    for peer in peers:
-        greet({"row": peer})
+    greet({"row": near})
     greet(mate)
     for copy in [obj_load] + probes + loads:
         copy.start()
     with mark("w_barrier"):
-        pl.semaphore_wait(
-            barrier, 1 + has_far.astype(jnp.int32) + passed.astype(jnp.int32) + passes.astype(jnp.int32) + len(peers)
-        )
+        pl.semaphore_wait(barrier, 2 + has_far.astype(jnp.int32))
+
+    rounds = [2]
+    while 4 * rounds[-1] < rows:
+        rounds.append(2 * rounds[-1])
+
+    def sides(r):
+        return (me - rounds[r], me - rounds[r] >= 0), (me + rounds[r], me + rounds[r] < rows)
+
+    def tell(r):
+        for row, there in sides(r):
+
+            @pl.when(there)
+            def _():
+                pl.semaphore_signal(news.at[r], inc=1, device_id={"row": row}, device_id_type=MESH)
+
+    def hear(r):
+        (_, above), (_, below) = sides(r)
+        pl.semaphore_wait(news.at[r], above.astype(jnp.int32) + below.astype(jnp.int32))
 
     def remote(src, dst, send, recv, to):
         return pltpu.make_async_remote_copy(
@@ -217,6 +229,7 @@
         for i in range(last):
             far_strip(i)
 
+    tell(0)
     obj_load.wait()
     for copy in loads:
         copy.wait()
@@ -326,6 +339,11 @@
                 p = k - pairs
                 with mark("w_partner"):
                     to_partner(p).wait_recv()
+                if p == 0:
+                    for r in range(len(rounds)):
+                        hear(r)
+                        if r + 1 < len(rounds):
+                            tell(r + 1)
                 acc[p] = term[k] + tpart[p]
                 for c in range(CUTS):
                     for hop in hops:
@@ -535,6 +553,7 @@
             dma((1,)), dma((pairs, CUTS, rounds)),
             dma((1,)), dma((pairs, CUTS)),
             dma((1,)), dma((pairs,)),
+            pltpu.SemaphoreType.REGULAR((rows.bit_length(),)),
         ],
         compiler_params=pltpu.CompilerParams(
             collective_id=0, has_side_effects=True, vmem_limit_bytes=24 << 20

time: 31.3 us -> 31 us (level)
    pallas_call x1, Pallas kernels: 29 us -> 28.6 us  [body(): pl.pallas_call(functools.partial(kernel, rows, modes, slots, n), out_shap...]
where the time goes in v4:
time: 31 us; the launch traced here: 30.8 us
  Pallas kernels  29.5 us (95%)
  between operations  1.29 us (4%)
    pallas_call x1, Pallas kernels, body(): pl.pallas_call(functools.partial(kernel, rows, modes, slots, n), out_shap...  28.6 us
    pallas_call x1, Pallas kernels, body(): pl.pallas_call(finish, out_shape=outs, in_specs=[vmem] * 2, out_specs=(hb...  0.87 us

profile of v4, /device:TPU:0, one launch (start us, length us, event | category | flops | bytes accessed | tf_op | source)
XLA Modules:
  0.0 30.8 jit_solution(13588643614993448615)
XLA Ops:
  1.3 28.6 %shard_map.77 = (f32[256,128]{1,0:T(8,128)S(1)}, f32[4,2,128,128]{3,2,1,0:T(8,128)S(1)}) custom-call(s32[1,1,2,2]{3,2,1,0:T(2,128)} %off_hbm.1, s32[1,1]{1,0:T(1,128)S(6)} %copy.8.cnt_hbm, f32[256,128]{1,0:T(8,128)} %bitcast.2, f32[4,2,128,128]{3,2,1,0:T(8,128)} %probe_hbm.1, f32[1,1,2,128,128]{4,3,2,1,0:T(8,128)} %pat_hbm.1, ...), custom_call_target="tpu_custom_call" | custom-call | tf_op jit(solution)/shard_map/pallas_call | solution.py:509
  29.9 0.9 %shard_map.78 = (f32[256,128]{1,0:T(8,128)}, f32[4,2,128,128]{3,2,1,0:T(8,128)}) custom-call(f32[256,128]{1,0:T(8,128)S(1)} %get-tuple-element.6.obj_ref, f32[4,2,128,128]{3,2,1,0:T(8,128)S(1)} %get-tuple-element.7.probe_ref), custom_call_target="tpu_custom_call" | custom-call | tf_op jit(solution)/shard_map/pallas_call | solution.py:562

commit v5 on v4

--- a/solution.py
+++ b/solution.py
@@ -68,6 +68,13 @@
     return group, ways
 
 
+def tells(rows):
+    distances = [2]
+    while 4 * distances[-1] < rows:
+        distances.append(2 * distances[-1])
+    return distances
+
+
 CUTS = 2
 STRIPS = (2, 2, 2, 1, 1)
 
@@ -78,9 +85,9 @@
     obj_out, probe_out,
     off_ref, cnt_ref, probe_ref, pat_ref, tab_ref,
     frame, xh, xl, yh, yl, far, vh, vl, win, gacc,
-    gown, gpar, grecv, gnear, gfar, gvia, term, tpart, acc, pieces, part, swapped, fin, fin_other,
-    load, hm_send, hm_recv, n_send, n_recv, f_send, f_recv, p_send, r_send, r_recv, g_send, g_recv,
-    e_send, e_recv, t_send, t_recv, rs_send, rs_recv, x_send, x_recv, ag_send, ag_recv, o_send, o_recv, news,
+    gown, gpar, grecv, gnear, gfar, gvia, tally, term, tpart, acc, pieces, part, swapped, fin, fin_other,
+    load, sent, sent_far, sent_on, hm_recv, n_recv, f_recv, r_recv, g_recv,
+    e_recv, t_recv, rs_recv, x_recv, ag_recv, o_recv, d_recv, news,
 ):
     me = lax.axis_index("row")
     col = lax.axis_index("col")
@@ -116,9 +123,9 @@
     loads = [
         pltpu.make_async_copy(off_hbm, off_ref, load.at[1]),
         pltpu.make_async_copy(cnt_hbm, cnt_ref, load.at[2]),
-        pltpu.make_async_copy(pat_hbm, pat_ref, load.at[3]),
-        pltpu.make_async_copy(tab_hbm, tab_ref, load.at[4]),
     ]
+    tables = pltpu.make_async_copy(tab_hbm, tab_ref, load.at[3])
+    pattern = pltpu.make_async_copy(pat_hbm, pat_ref, load.at[4])
     probes = [pltpu.make_async_copy(probe_hbm.at[mode_at(j)], probe_ref.at[j], load.at[5]) for j in range(modes)]
     all_probes = pltpu.make_async_copy(probe_hbm, probe_ref, load.at[5])
 
@@ -130,14 +137,12 @@
     pl.when(has_far)(lambda: greet({"row": far_row}))
     greet({"row": near})
     greet(mate)
-    for copy in [obj_load] + probes + loads:
+    for copy in [obj_load] + probes + loads + [tables, pattern]:
         copy.start()
     with mark("w_barrier"):
         pl.semaphore_wait(barrier, 2 + has_far.astype(jnp.int32))
 
-    rounds = [2]
-    while 4 * rounds[-1] < rows:
-        rounds.append(2 * rounds[-1])
+    rounds = tells(rows)
 
     def sides(r):
         return (me - rounds[r], me - rounds[r] >= 0), (me + rounds[r], me + rounds[r] < rows)
@@ -163,25 +168,25 @@
     unit = 2 * n // sum(STRIPS)
     starts = [unit * sum(STRIPS[:i]) for i in range(len(STRIPS) + 1)]
     strips = [pl.ds(starts[i], starts[i + 1] - starts[i]) for i in range(len(STRIPS))]
-    to_mate = remote(obj_hbm, frame.at[1, seen], hm_send.at[0], hm_recv.at[0], mate)
+    to_mate = remote(obj_hbm, frame.at[1, seen], sent.at[0], hm_recv.at[0], mate)
 
     def to_near(i, at=None):
         at = strips[i] if at is None else at
-        return remote(obj_hbm.at[at], frame.at[far_at, 1, at], n_send.at[0], n_recv.at[i], {"row": near})
+        return remote(obj_hbm.at[at], frame.at[far_at, 1, at], sent.at[0], n_recv.at[i], {"row": near})
 
     def to_far(i, at=None):
         at = strips[i] if at is None else at
-        return remote(obj_hbm.at[at], frame.at[near_at, 1, at], f_send.at[0], f_recv.at[i], {"row": far_row})
+        return remote(obj_hbm.at[at], frame.at[near_at, 1, at], sent_on.at[0], f_recv.at[i], {"row": far_row})
 
     def pass_on(i, at=None):
         at = strips[i] if at is None else at
         return remote(
-            frame.at[near_at, 1, at], frame.at[far_at, 1, at], p_send.at[0], f_recv.at[i], {"row": behind}
+            frame.at[near_at, 1, at], frame.at[far_at, 1, at], sent_on.at[0], f_recv.at[i], {"row": behind}
         )
 
     def relay(block, kind, at):
         return remote(
-            frame.at[block, 1, at], frame.at[block, seen, at], r_send.at[kind], r_recv.at[kind], mate
+            frame.at[block, 1, at], frame.at[block, seen, at], (sent, sent_far)[kind].at[0], r_recv.at[kind], mate
         )
 
     whole = pl.ds(0, 2 * n)
@@ -231,7 +236,7 @@
 
     tell(0)
     obj_load.wait()
-    for copy in loads:
+    for copy in loads + [tables, pattern]:
         copy.wait()
     to_mate.wait_recv()
     with mark("w_relay"):
@@ -293,7 +298,7 @@
                 yl[spot] = lo
 
     def to_partner(p):
-        return remote(term.at[p], tpart.at[p], t_send.at[0], t_recv.at[p], mate)
+        return remote(term.at[p], tpart.at[p], sent.at[0], t_recv.at[p], mate)
 
     def rows_of(owner, c):
         return pl.ds(pl.multiple_of(owner * slab + c * chunk, 8), chunk)
@@ -301,7 +306,7 @@
     def scatter(p, c, hop):
         return remote(
             acc.at[p, rows_of(hop_to(seat, hop), c)], pieces.at[p, c, hop - 1],
-            rs_send.at[0], rs_recv.at[p, c], {"row": hop_to(me, hop)},
+            sent.at[0], rs_recv.at[p, c], {"row": hop_to(me, hop)},
         )
 
     hops = list(range(1, group))
@@ -350,7 +355,7 @@
                         scatter(p, c, hop).start()
 
     def across(j):
-        return remote(gpar.at[j], grecv.at[j], g_send.at[0], g_recv.at[j], mate)
+        return remote(gpar.at[j], grecv.at[j], sent.at[0], g_recv.at[j], mate)
 
     for q in range(2):
         own = [jnp.zeros((n, n), F32)] * 3
@@ -371,9 +376,9 @@
         for j in range(3):
             gown[j, q * n : (q + 1) * n] = own[j]
             gpar[j, q * n : (q + 1) * n] = par[j]
-    edge_far = remote(gown.at[far_at], gfar, e_send.at[0], e_recv.at[0], {"row": far_row})
-    edge_via = remote(gown.at[far_at], gvia, e_send.at[0], e_recv.at[2], {"row": beyond})
-    edge_near = remote(gown.at[near_at], gnear, e_send.at[1], e_recv.at[1], {"row": near})
+    edge_far = remote(gown.at[far_at], gfar, sent_far.at[0], e_recv.at[0], {"row": far_row})
+    edge_via = remote(gown.at[far_at], gvia, sent_far.at[0], e_recv.at[2], {"row": beyond})
+    edge_near = remote(gown.at[near_at], gnear, sent.at[0], e_recv.at[1], {"row": near})
     for j in (far_at, near_at, 1):
         across(j).start()
     with mark("w_across"):
@@ -386,16 +391,22 @@
 
     def exchange(r, p, c):
         return remote(
-            part.at[p, c, r], swapped.at[p, c, r], x_send.at[0], x_recv.at[p, c, r], {"row": flip(me, ways[r])}
+            part.at[p, c, r], swapped.at[p, c, r], sent.at[0], x_recv.at[p, c, r], {"row": flip(me, ways[r])}
         )
 
     def gather(p, c, hop):
         here = fin.at[p, rows_of(seat, c)]
-        return remote(here, here, ag_send.at[0], ag_recv.at[p, c], {"row": hop_to(me, hop)})
+        return remote(here, here, sent.at[0], ag_recv.at[p, c], {"row": hop_to(me, hop)})
+
+    def gather_other(p, c, hop):
+        return remote(
+            fin.at[p, rows_of(seat, c)], fin_other.at[p, rows_of(seat, c)], sent.at[0], d_recv.at[0],
+            {"row": hop_to(me, hop), "col": 1 - col},
+        )
 
     def share(p, c, hop):
         at = rows_of(hop_to(seat, hop), c)
-        return remote(fin.at[p, at], fin_other.at[p, at], o_send.at[0], o_recv.at[p], mate)
+        return remote(fin.at[p, at], fin_other.at[p, at], sent.at[0], o_recv.at[p], mate)
 
     def settle(r, p, c, total):
         if r < len(ways):
@@ -405,15 +416,17 @@
             fin[p, rows_of(seat, c)] = total
             for hop in hops:
                 gather(p, c, hop).start()
+                if (p, c) == chunks[-1]:
+                    gather_other(p, c, hop).start()
             share(p, c, 0).start()
 
-    def all_of(ref, send, recv):
-        return remote(ref, ref, send, recv, mate)
+    def all_of(ref, recv):
+        return remote(ref, ref, sent.at[0], recv, mate)
 
     for p, c in chunks:
         total = acc[p, rows_of(seat, c)]
         with mark("w_rs"):
-            all_of(pieces.at[p, c], rs_send.at[0], rs_recv.at[p, c]).wait_recv()
+            all_of(pieces.at[p, c], rs_recv.at[p, c]).wait_recv()
         for hop in hops:
             total = total + pieces[p, c, hop - 1]
         settle(0, p, c, total)
@@ -437,9 +450,10 @@
 
     for p, c in chunks:
         with mark("w_ag"):
-            all_of(pieces.at[p, c], ag_send.at[0], ag_recv.at[p, c]).wait_recv()
+            all_of(pieces.at[p, c], ag_recv.at[p, c]).wait_recv()
         for hop in hops:
-            share(p, c, hop).start()
+            if (p, c) != chunks[-1]:
+                share(p, c, hop).start()
     for p in range(pairs):
         for q in range(2):
             half = slice(q * n, (q + 1) * n)
@@ -455,27 +469,25 @@
 
     for p in range(pairs):
         with mark("w_share"):
-            all_of(fin_other.at[p], o_send.at[0], o_recv.at[p]).wait_recv()
+            if p < pairs - 1:
+                all_of(fin_other.at[p], o_recv.at[p]).wait_recv()
+            else:
+                rest = pl.ds(0, 2 * n - (group - 1) * chunk)
+                all_of(fin_other.at[p, rest], o_recv.at[p]).wait_recv()
+                if hops:
+                    all_of(pieces.at[0, 0], d_recv.at[0]).wait_recv()
         for q in range(2):
             half = slice(q * n, (q + 1) * n)
             probe_out[2 * p + 1 - col, q] = probe_ref[p, q] - probe_rate * fin_other[p, half] / tiles
 
     with mark("w_sends"):
-        to_mate.wait_send()
-        to_near(0, whole).wait_send()
-        pl.when(direct)(to_far(0, whole).wait_send)
-        pl.when(passes)(pass_on(0, whole).wait_send)
-        relay(near_at, 0, whole).wait_send()
-        pl.when(has_far)(relay(far_at, 1, whole).wait_send)
-        pl.when(has_far)(edge_far.wait_send)
-        edge_near.wait_send()
-        for ref, send, recv in (
-            (tpart, t_send, t_recv.at[0]), (gpar, g_send, g_recv.at[0]), (pieces, rs_send, rs_recv.at[0, 0]),
-            (pieces, ag_send, ag_recv.at[0, 0]), (fin_other, o_send, o_recv.at[0]),
-        ):
-            all_of(ref, send.at[0], recv).wait_send()
-        if ways:
-            all_of(part, x_send.at[0], x_recv.at[0, 0, 0]).wait_send()
+        def drain(count, sem):
+            here = tally.at[pl.ds(0, count)]
+            remote(here, here, sem.at[0], hm_recv.at[0], mate).wait_send()
+
+        drain(tally.shape[0], sent)
+        pl.when(has_far)(lambda: drain(4 * n, sent_far))
+        pl.when(jnp.logical_or(direct, passes))(lambda: drain(2 * n, sent_on))
 
 
 def finish(obj_ref, probe_ref, obj_out, probe_out, sem):
@@ -497,6 +509,7 @@
     block = object_field.reshape(2 * n, n)
     rounds = max(1, len(ways))
     chunk = 2 * n // group // CUTS
+    rows_sent = 2 * n * (4 + pairs + 3 + pairs) + pairs * CUTS * chunk * (2 * (group - 1) + len(ways))
     tables = jnp.asarray(dft_tables(n))
     vmem = pl.BlockSpec(memory_space=pltpu.VMEM)
     hbm = pl.BlockSpec(memory_space=pltpu.HBM)
@@ -533,6 +546,7 @@
             pltpu.VMEM((2 * n, n), F32),
             pltpu.VMEM((2 * n, n), F32),
             pltpu.VMEM((2 * n, n), F32),
+            pltpu.VMEM((rows_sent, n), F32),
             pltpu.VMEM((modes, 2 * n, n), F32),
             pltpu.VMEM((pairs, 2 * n, n), F32),
             pltpu.VMEM((pairs, 2 * n, n), F32),
@@ -541,19 +555,11 @@
             pltpu.VMEM((pairs, CUTS, rounds, chunk, n), F32),
             pltpu.VMEM((pairs, 2 * n, n), F32),
             pltpu.VMEM((pairs, 2 * n, n), F32),
-            dma((6,)),
-            dma((1,)), dma((1,)),
-            dma((1,)), dma((len(STRIPS),)),
-            dma((1,)), dma((len(STRIPS),)), dma((1,)),
-            dma((2,)), dma((2,)),
-            dma((1,)), dma((3,)),
-            dma((2,)), dma((3,)),
-            dma((1,)), dma((pairs,)),
-            dma((1,)), dma((pairs, CUTS)),
-            dma((1,)), dma((pairs, CUTS, rounds)),
-            dma((1,)), dma((pairs, CUTS)),
-            dma((1,)), dma((pairs,)),
-            pltpu.SemaphoreType.REGULAR((rows.bit_length(),)),
+            dma((6,)), dma((1,)), dma((1,)), dma((1,)),
+            dma((1,)), dma((len(STRIPS),)), dma((len(STRIPS),)), dma((2,)), dma((3,)),
+            dma((3,)), dma((pairs,)), dma((pairs, CUTS)), dma((pairs, CUTS, rounds)),
+            dma((pairs, CUTS)), dma((pairs,)), dma((1,)),
+            pltpu.SemaphoreType.REGULAR((len(tells(rows)),)),
         ],
         compiler_params=pltpu.CompilerParams(
             collective_id=0, has_side_effects=True, vmem_limit_bytes=24 << 20

time: 31 us -> 30.3 us (0.977)
  Pallas kernels: 29.5 us -> 28.9 us
    pallas_call x1, Pallas kernels: 28.6 us -> 28 us  [body(): pl.pallas_call(functools.partial(kernel, rows, modes, slots, n), out_shap...]
where the time goes in v5:
time: 30.3 us; the launch traced here: 30.1 us
  Pallas kernels  28.9 us (95%)
  between operations  1.29 us (4%)
    pallas_call x1, Pallas kernels, body(): pl.pallas_call(functools.partial(kernel, rows, modes, slots, n), out_shap...  28 us
    pallas_call x1, Pallas kernels, body(): pl.pallas_call(finish, out_shape=outs, in_specs=[vmem] * 2, out_specs=(hb...  0.87 us

profile of v5, /device:TPU:0, one launch (start us, length us, event | category | flops | bytes accessed | tf_op | source)
XLA Modules:
  0.0 30.1 jit_solution(7587409525986701922)
XLA Ops:
  1.3 28.0 %shard_map.77 = (f32[256,128]{1,0:T(8,128)S(1)}, f32[4,2,128,128]{3,2,1,0:T(8,128)S(1)}) custom-call(s32[1,1,2,2]{3,2,1,0:T(2,128)} %off_hbm.1, s32[1,1]{1,0:T(1,128)S(6)} %copy.8.cnt_hbm, f32[256,128]{1,0:T(8,128)} %bitcast.2, f32[4,2,128,128]{3,2,1,0:T(8,128)} %probe_hbm.1, f32[1,1,2,128,128]{4,3,2,1,0:T(8,128)} %pat_hbm.1, ...), custom_call_target="tpu_custom_call" | custom-call | tf_op jit(solution)/shard_map/pallas_call | solution.py:522
  29.3 0.9 %shard_map.78 = (f32[256,128]{1,0:T(8,128)}, f32[4,2,128,128]{3,2,1,0:T(8,128)}) custom-call(f32[256,128]{1,0:T(8,128)S(1)} %get-tuple-element.6.obj_ref, f32[4,2,128,128]{3,2,1,0:T(8,128)S(1)} %get-tuple-element.7.probe_ref), custom_call_target="tpu_custom_call" | custom-call | tf_op jit(solution)/shard_map/pallas_call | solution.py:568

commit v6 on v5

--- a/solution.py
+++ b/solution.py
@@ -76,7 +76,7 @@
 
 
 CUTS = 2
-STRIPS = (2, 2, 2, 1, 1)
+STRIPS = (3, 3, 2)
 
 
 def kernel(
@@ -351,7 +351,7 @@
                             tell(r + 1)
                 acc[p] = term[k] + tpart[p]
                 for c in range(CUTS):
-                    for hop in hops:
+                    for hop in hops[::-1]:
                         scatter(p, c, hop).start()
 
     def across(j):

time: 30.3 us -> 30 us (0.990)
  no operation moved by 1% of the time
where the time goes in v6:
time: 30 us; the launch traced here: 29.9 us
  Pallas kernels  28.6 us (95%)
  between operations  1.29 us (4%)
    pallas_call x1, Pallas kernels, body(): pl.pallas_call(functools.partial(kernel, rows, modes, slots, n), out_shap...  27.7 us
    pallas_call x1, Pallas kernels, body(): pl.pallas_call(finish, out_shape=outs, in_specs=[vmem] * 2, out_specs=(hb...  0.87 us

profile of v6, /device:TPU:0, one launch (start us, length us, event | category | flops | bytes accessed | tf_op | source)
XLA Modules:
  0.0 29.9 jit_solution(16686340915278162595)
XLA Ops:
  1.3 27.7 %shard_map.77 = (f32[256,128]{1,0:T(8,128)S(1)}, f32[4,2,128,128]{3,2,1,0:T(8,128)S(1)}) custom-call(s32[1,1,2,2]{3,2,1,0:T(2,128)} %off_hbm.1, s32[1,1]{1,0:T(1,128)S(6)} %copy.8.cnt_hbm, f32[256,128]{1,0:T(8,128)} %bitcast.2, f32[4,2,128,128]{3,2,1,0:T(8,128)} %probe_hbm.1, f32[1,1,2,128,128]{4,3,2,1,0:T(8,128)} %pat_hbm.1, ...), custom_call_target="tpu_custom_call" | custom-call | tf_op jit(solution)/shard_map/pallas_call | solution.py:522
  29.0 0.9 %shard_map.78 = (f32[256,128]{1,0:T(8,128)}, f32[4,2,128,128]{3,2,1,0:T(8,128)}) custom-call(f32[256,128]{1,0:T(8,128)S(1)} %get-tuple-element.6.obj_ref, f32[4,2,128,128]{3,2,1,0:T(8,128)S(1)} %get-tuple-element.7.probe_ref), custom_call_target="tpu_custom_call" | custom-call | tf_op jit(solution)/shard_map/pallas_call | solution.py:568

commit v7 on v6

--- a/solution.py
+++ b/solution.py
@@ -87,7 +87,7 @@
     frame, xh, xl, yh, yl, far, vh, vl, win, gacc,
     gown, gpar, grecv, gnear, gfar, gvia, tally, term, tpart, acc, pieces, part, swapped, fin, fin_other,
     load, sent, sent_far, sent_on, hm_recv, n_recv, f_recv, r_recv, g_recv,
-    e_recv, t_recv, rs_recv, x_recv, ag_recv, o_recv, d_recv, news,
+    e_recv, t_recv, rs_recv, x_recv, ag_recv, o_recv, news,
 ):
     me = lax.axis_index("row")
     col = lax.axis_index("col")
@@ -124,10 +124,10 @@
         pltpu.make_async_copy(off_hbm, off_ref, load.at[1]),
         pltpu.make_async_copy(cnt_hbm, cnt_ref, load.at[2]),
     ]
-    tables = pltpu.make_async_copy(tab_hbm, tab_ref, load.at[3])
-    pattern = pltpu.make_async_copy(pat_hbm, pat_ref, load.at[4])
-    probes = [pltpu.make_async_copy(probe_hbm.at[mode_at(j)], probe_ref.at[j], load.at[5]) for j in range(modes)]
-    all_probes = pltpu.make_async_copy(probe_hbm, probe_ref, load.at[5])
+    tables = pltpu.make_async_copy(tab_hbm, tab_ref, load.at[0])
+    pattern = pltpu.make_async_copy(pat_hbm, pat_ref, load.at[0])
+    probes = [pltpu.make_async_copy(probe_hbm.at[mode_at(j)], probe_ref.at[j], load.at[3]) for j in range(modes)]
+    all_probes = pltpu.make_async_copy(probe_hbm, probe_ref, load.at[3])
 
     barrier = pltpu.get_barrier_semaphore()
 
@@ -235,9 +235,10 @@
             far_strip(i)
 
     tell(0)
-    obj_load.wait()
-    for copy in loads + [tables, pattern]:
+    for copy in loads:
         copy.wait()
+    loaded = tally.at[pl.ds(0, 2 * n + pat_ref.shape[2] * n + 8 * n)]
+    pltpu.make_async_copy(loaded, loaded, load.at[0]).wait()
     to_mate.wait_recv()
     with mark("w_relay"):
         relay(near_at, 0, whole).wait_recv()
@@ -400,7 +401,7 @@
 
     def gather_other(p, c, hop):
         return remote(
-            fin.at[p, rows_of(seat, c)], fin_other.at[p, rows_of(seat, c)], sent.at[0], d_recv.at[0],
+            fin.at[p, rows_of(seat, c)], fin_other.at[p, rows_of(seat, c)], sent.at[0], o_recv.at[p],
             {"row": hop_to(me, hop), "col": 1 - col},
         )
 
@@ -457,7 +458,7 @@
     for p in range(pairs):
         for q in range(2):
             half = slice(q * n, (q + 1) * n)
-            probe_out[2 * p + col, q] = probe_ref[pairs + p, q] - probe_rate * fin[p, half] / tiles
+            probe_out[2 * p + col, q] = probe_ref[pairs + p, q] - (probe_rate / tiles) * fin[p, half]
     with mark("w_edge"):
         across(1).wait_recv()
         edge_near.wait_recv()
@@ -469,16 +470,10 @@
 
     for p in range(pairs):
         with mark("w_share"):
-            if p < pairs - 1:
-                all_of(fin_other.at[p], o_recv.at[p]).wait_recv()
-            else:
-                rest = pl.ds(0, 2 * n - (group - 1) * chunk)
-                all_of(fin_other.at[p, rest], o_recv.at[p]).wait_recv()
-                if hops:
-                    all_of(pieces.at[0, 0], d_recv.at[0]).wait_recv()
+            all_of(fin_other.at[p], o_recv.at[p]).wait_recv()
         for q in range(2):
             half = slice(q * n, (q + 1) * n)
-            probe_out[2 * p + 1 - col, q] = probe_ref[p, q] - probe_rate * fin_other[p, half] / tiles
+            probe_out[2 * p + 1 - col, q] = probe_ref[p, q] - (probe_rate / tiles) * fin_other[p, half]
 
     with mark("w_sends"):
         def drain(count, sem):
@@ -555,10 +550,10 @@
             pltpu.VMEM((pairs, CUTS, rounds, chunk, n), F32),
             pltpu.VMEM((pairs, 2 * n, n), F32),
             pltpu.VMEM((pairs, 2 * n, n), F32),
-            dma((6,)), dma((1,)), dma((1,)), dma((1,)),
+            dma((4,)), dma((1,)), dma((1,)), dma((1,)),
             dma((1,)), dma((len(STRIPS),)), dma((len(STRIPS),)), dma((2,)), dma((3,)),
             dma((3,)), dma((pairs,)), dma((pairs, CUTS)), dma((pairs, CUTS, rounds)),
-            dma((pairs, CUTS)), dma((pairs,)), dma((1,)),
+            dma((pairs, CUTS)), dma((pairs,)),
             pltpu.SemaphoreType.REGULAR((len(tells(rows)),)),
         ],
         compiler_params=pltpu.CompilerParams(

time: 30 us -> 30 us (level)
  no operation moved by 1% of the time
where the time goes in v7:
time: 30 us; the launch traced here: 29.8 us
  Pallas kernels  28.5 us (95%)
  between operations  1.29 us (4%)
    pallas_call x1, Pallas kernels, body(): pl.pallas_call(functools.partial(kernel, rows, modes, slots, n), out_shap...  27.7 us
    pallas_call x1, Pallas kernels, body(): pl.pallas_call(finish, out_shape=outs, in_specs=[vmem] * 2, out_specs=(hb...  0.87 us

profile of v7, /device:TPU:0, one launch (start us, length us, event | category | flops | bytes accessed | tf_op | source)
XLA Modules:
  0.0 29.8 jit_solution(4127140880257044309)
XLA Ops:
  1.3 27.7 %shard_map.77 = (f32[256,128]{1,0:T(8,128)S(1)}, f32[4,2,128,128]{3,2,1,0:T(8,128)S(1)}) custom-call(s32[1,1,2,2]{3,2,1,0:T(2,128)} %off_hbm.1, s32[1,1]{1,0:T(1,128)S(6)} %copy.8.cnt_hbm, f32[256,128]{1,0:T(8,128)} %bitcast.2, f32[4,2,128,128]{3,2,1,0:T(8,128)} %probe_hbm.1, f32[1,1,2,128,128]{4,3,2,1,0:T(8,128)} %pat_hbm.1, ...), custom_call_target="tpu_custom_call" | custom-call | tf_op jit(solution)/shard_map/pallas_call | solution.py:517
  29.0 0.9 %shard_map.78 = (f32[256,128]{1,0:T(8,128)}, f32[4,2,128,128]{3,2,1,0:T(8,128)}) custom-call(f32[256,128]{1,0:T(8,128)S(1)} %get-tuple-element.6.obj_ref, f32[4,2,128,128]{3,2,1,0:T(8,128)S(1)} %get-tuple-element.7.probe_ref), custom_call_target="tpu_custom_call" | custom-call | tf_op jit(solution)/shard_map/pallas_call | solution.py:563

commit v8 on v7

--- a/solution.py
+++ b/solution.py
@@ -86,7 +86,7 @@
     off_ref, cnt_ref, probe_ref, pat_ref, tab_ref,
     frame, xh, xl, yh, yl, far, vh, vl, win, gacc,
     gown, gpar, grecv, gnear, gfar, gvia, tally, term, tpart, acc, pieces, part, swapped, fin, fin_other,
-    load, sent, sent_far, sent_on, hm_recv, n_recv, f_recv, r_recv, g_recv,
+    load, sent, sent_far, sent_on, n_recv, f_recv, r_recv, g_recv,
     e_recv, t_recv, rs_recv, x_recv, ag_recv, o_recv, news,
 ):
     me = lax.axis_index("row")
@@ -168,7 +168,7 @@
     unit = 2 * n // sum(STRIPS)
     starts = [unit * sum(STRIPS[:i]) for i in range(len(STRIPS) + 1)]
     strips = [pl.ds(starts[i], starts[i + 1] - starts[i]) for i in range(len(STRIPS))]
-    to_mate = remote(obj_hbm, frame.at[1, seen], sent.at[0], hm_recv.at[0], mate)
+    to_mate = remote(obj_hbm, frame.at[1, seen], sent.at[0], r_recv.at[0], mate)
 
     def to_near(i, at=None):
         at = strips[i] if at is None else at
@@ -239,9 +239,9 @@
         copy.wait()
     loaded = tally.at[pl.ds(0, 2 * n + pat_ref.shape[2] * n + 8 * n)]
     pltpu.make_async_copy(loaded, loaded, load.at[0]).wait()
-    to_mate.wait_recv()
     with mark("w_relay"):
-        relay(near_at, 0, whole).wait_recv()
+        both = tally.at[pl.ds(0, 4 * n)]
+        remote(both, both, sent.at[0], r_recv.at[0], mate).wait_recv()
         pl.when(has_far)(relay(far_at, 1, whole).wait_recv)
 
     r_hi, r_lo, l_hi, l_lo = (tab_ref.at[t] for t in range(4))
@@ -478,7 +478,7 @@
     with mark("w_sends"):
         def drain(count, sem):
             here = tally.at[pl.ds(0, count)]
-            remote(here, here, sem.at[0], hm_recv.at[0], mate).wait_send()
+            remote(here, here, sem.at[0], r_recv.at[0], mate).wait_send()
 
         drain(tally.shape[0], sent)
         pl.when(has_far)(lambda: drain(4 * n, sent_far))
@@ -551,7 +551,7 @@
             pltpu.VMEM((pairs, 2 * n, n), F32),
             pltpu.VMEM((pairs, 2 * n, n), F32),
             dma((4,)), dma((1,)), dma((1,)), dma((1,)),
-            dma((1,)), dma((len(STRIPS),)), dma((len(STRIPS),)), dma((2,)), dma((3,)),
+            dma((len(STRIPS),)), dma((len(STRIPS),)), dma((2,)), dma((3,)),
             dma((3,)), dma((pairs,)), dma((pairs, CUTS)), dma((pairs, CUTS, rounds)),
             dma((pairs, CUTS)), dma((pairs,)),
             pltpu.SemaphoreType.REGULAR((len(tells(rows)),)),

time: 30 us -> 30 us (level)
  no operation moved by 1% of the time
where the time goes in v8:
time: 30 us; the launch traced here: 29.8 us
  Pallas kernels  28.5 us (95%)
  between operations  1.29 us (4%)
    pallas_call x1, Pallas kernels, body(): pl.pallas_call(functools.partial(kernel, rows, modes, slots, n), out_shap...  27.7 us
    pallas_call x1, Pallas kernels, body(): pl.pallas_call(finish, out_shape=outs, in_specs=[vmem] * 2, out_specs=(hb...  0.87 us

profile of v8, /device:TPU:0, one launch (start us, length us, event | category | flops | bytes accessed | tf_op | source)
XLA Modules:
  0.0 29.8 jit_solution(16961878697374711710)
XLA Ops:
  1.3 27.7 %shard_map.77 = (f32[256,128]{1,0:T(8,128)S(1)}, f32[4,2,128,128]{3,2,1,0:T(8,128)S(1)}) custom-call(s32[1,1,2,2]{3,2,1,0:T(2,128)} %off_hbm.1, s32[1,1]{1,0:T(1,128)S(6)} %copy.8.cnt_hbm, f32[256,128]{1,0:T(8,128)} %bitcast.2, f32[4,2,128,128]{3,2,1,0:T(8,128)} %probe_hbm.1, f32[1,1,2,128,128]{4,3,2,1,0:T(8,128)} %pat_hbm.1, ...), custom_call_target="tpu_custom_call" | custom-call | tf_op jit(solution)/shard_map/pallas_call | solution.py:517
  29.0 0.9 %shard_map.78 = (f32[256,128]{1,0:T(8,128)}, f32[4,2,128,128]{3,2,1,0:T(8,128)}) custom-call(f32[256,128]{1,0:T(8,128)S(1)} %get-tuple-element.6.obj_ref, f32[4,2,128,128]{3,2,1,0:T(8,128)S(1)} %get-tuple-element.7.probe_ref), custom_call_target="tpu_custom_call" | custom-call | tf_op jit(solution)/shard_map/pallas_call | solution.py:563
